TPU v7x, 512 devices: a whole 4x8x8 slice. The times are simulated.
512 devices in a mesh: row: 32 (over z, x), col: 16 (over y, core).
Axes of the slice: x: 4, y: 8, z: 8, core: 2. Of those that a mesh axis runs over, the one named last changes fastest.
Arguments:
- field: bfloat16 [1, 64, 2048, 2048], P(None, None, 'row', 'col'), may hold values from -6 to 6
- x_weight: float32 [2, 2, 12, 64, 64], replicated, may hold values from -2 to 2
- y_weight: float32 [2, 2, 12, 64, 64], replicated, may hold values from -2 to 2
- up_weight: bfloat16 [2, 256, 64], replicated, may hold values from -0.75 to 0.75
- up_bias: float32 [2, 256], replicated, may hold values from -3 to 3
- down_weight: bfloat16 [2, 64, 256], replicated, may hold values from -0.375 to 0.375
Outputs:
- result: bfloat16 [1, 64, 2048, 2048], P(None, None, 'row', 'col')
All inputs are finite; a program needn't handle non-finite values.
Results may differ from a plain program's by a relative error of at most 0.025.
Values may be sent and summed in bfloat16 or wider, within the bound.
No kernel may reach another device: no remote copies, remote signals or barrier semaphores. Data moves between devices by JAX's collectives and lax.ppermute only.
A program may use at most 64 MiB of HBM per device.

v0:
```python
import functools
import math

import jax
import jax.numpy as jnp
from jax import lax
from jax.experimental import pallas as pl
from jax.experimental.pallas import tpu as pltpu
from jax.sharding import PartitionSpec as P


MODES = 12
ROWS = 2 * MODES
LAYERS = 2
ROOT_HALF = math.sqrt(0.5)
NN = (((1,), (0,)), ((), ()))
TN = (((0,), (0,)), ((), ()))
NT = (((1,), (1,)), ((), ()))
F32, BF16 = jnp.float32, jnp.bfloat16
BLOCK = 4
WIDE = 4
AHEAD = 2
PAD = 8
EXTRA = 16


def dot(a, b, dims=NN):
    return lax.dot_general(a, b, dims, preferred_element_type=F32)


def angles(total, start, count):
    pos = start + jnp.arange(count, dtype=jnp.int32)
    kays = jnp.arange(MODES, dtype=jnp.int32)
    phase = kays[:, None] * pos[None, :] % total
    angle = phase.astype(F32) * (2.0 * math.pi / total)
    wave = jnp.concatenate([jnp.cos(angle), -jnp.sin(angle)], axis=0)
    once = jnp.concatenate([kays, kays]) == 0
    factor = (jnp.where(once, 1.0, 2.0) / total).astype(F32)[:, None]
    return wave.astype(BF16), (wave * factor).astype(BF16)


def tables(nx, ny):
    fwd_x, inv_x = angles(nx * lax.axis_size("row"), lax.axis_index("row") * nx, nx)
    fwd_y, inv_y = angles(ny * lax.axis_size("col"), lax.axis_index("col") * ny, ny)
    return jnp.concatenate([fwd_y, inv_y, jnp.concatenate([fwd_x, inv_x], axis=1)], axis=0)


def put(ref, start, size, stride, value):
    ref[pl.ds(start, size, stride=stride), :] = value


def mixer(weight, k):
    real, imag = weight[0, k], weight[1, k]
    top = jnp.concatenate([real, imag], axis=1)
    bottom = jnp.concatenate([-imag, real], axis=1)
    return jnp.concatenate([top, bottom], axis=0).astype(BF16)


def forward_x(state, tab, got, weight, out, work, laid):
    chans, nx, ny = state.shape
    step = work.shape[0] // ROWS
    fwd = tab[2 * ROWS : 3 * ROWS, :nx].astype(F32)
    zero = jnp.zeros_like(fwd)
    lines = []
    for i in range(BLOCK):
        lines.append(jnp.concatenate([fwd if a == i else zero for a in range(BLOCK)], axis=1))
    table = jnp.concatenate(lines, axis=0).astype(BF16)
    for c0 in range(0, chans, BLOCK):
        part = dot(table, state[c0 : c0 + BLOCK].reshape(BLOCK * nx, ny))
        for i in range(BLOCK):
            put(work, c0 + i, ROWS, step, part[i * ROWS : (i + 1) * ROWS])
    got.wait()
    for k in range(MODES):
        re = work[k * step : k * step + chans]
        im = work[(MODES + k) * step : (MODES + k) * step + chans]
        mixed = dot(mixer(weight, k), jnp.concatenate([re, im], axis=0).astype(BF16), TN)
        put(laid, k, chans, ROWS, mixed[:chans])
        put(laid, MODES + k, chans, ROWS, mixed[chans:])
    out[...] = laid[...].astype(BF16)


def forward_y(state, tab, got, weight, out, work, laid):
    chans, nx, _ = state.shape
    half = chans // 2
    step = work.shape[0] // ROWS
    table = tab[:ROWS]
    for j in range(0, half, 2):
        both = [state[j], state[j + half], state[j + 1], state[j + 1 + half]]
        part = dot(table, jnp.concatenate(both, axis=0), NT)
        put(work, j, ROWS, step, part[:, : 2 * nx])
        put(work, j + 1, ROWS, step, part[:, 2 * nx :])
    got.wait()
    for k in range(MODES):
        re = work[k * step : k * step + half]
        im = work[(MODES + k) * step : (MODES + k) * step + half]
        stack = jnp.concatenate([re[:, :nx], re[:, nx:], im[:, :nx], im[:, nx:]], axis=0)
        mixed = dot(mixer(weight, k), stack.astype(BF16), TN)
        re = jnp.concatenate([mixed[:half], mixed[half:chans]], axis=1)
        im = jnp.concatenate([mixed[chans : chans + half], mixed[chans + half :]], axis=1)
        put(laid, k, half, ROWS, re)
        put(laid, MODES + k, half, ROWS, im)
    out[...] = laid[...].astype(BF16)


def add_branches(field, got_x, got_y, tab, tmp):
    chans, nx, _ = field.shape
    half = chans // 2
    step = tmp.shape[0] // chans
    to_y = tab[ROWS : 2 * ROWS]
    to_x = tab[2 * ROWS : 3 * ROWS, nx : 2 * nx].astype(F32).T.astype(BF16)
    for j in range(half):
        from_y = dot(got_y[j], to_y, TN)
        for h in range(2):
            c = j + h * half
            back = dot(to_x, got_x[c]) + from_y[h * nx : (h + 1) * nx]
            total = (field[c].astype(F32) + back).astype(BF16)
            tmp[c * step : c * step + nx] = total.astype(F32)


def feed_forward(layer, up, bias, down, tmp, lifted, nx):
    _, depth, hid = up.shape
    ny = tmp.shape[1]
    step = tmp.shape[0] // depth
    rest = bias[layer : layer + 1, :]
    rows = [up[layer].astype(F32)]
    for _ in range(3):
        part = rest.astype(BF16).astype(F32)
        rows.append(part)
        rest = rest - part
    rows.append(jnp.zeros((EXTRA - 3, hid), F32))
    lifted[...] = jnp.concatenate(rows, axis=0).T.astype(BF16)
    ones = (lax.broadcasted_iota(jnp.int32, (EXTRA, WIDE * ny), 0) < 3).astype(F32).astype(BF16)

    def feed(i, carry):
        x0 = i * (WIDE * AHEAD)
        wides, news = [], []
        for b in range(AHEAD):
            lines = [tmp[pl.ds(x0 + b * WIDE + a, depth, stride=step), :] for a in range(WIDE)]
            wides.append(jnp.concatenate(lines, axis=1))
        for wide in wides:
            hidden = dot(lifted[...], jnp.concatenate([wide.astype(BF16), ones], axis=0))
            hidden = hidden + hidden * lax.erf(hidden * ROOT_HALF)
            back = dot(down[layer] * jnp.asarray(0.5, BF16), hidden.astype(BF16))
            news.append((wide + back).astype(BF16).astype(F32))
        for b in range(AHEAD):
            for a in range(WIDE):
                line = news[b][:, a * ny : (a + 1) * ny]
                put(tmp, x0 + b * WIDE + a, depth, step, line)
        return carry

    lax.fori_loop(0, nx // (WIDE * AHEAD), feed, 0)


def fetch(source, target, sem):
    return pltpu.make_async_copy(source, target, sem)


def first_kernel(field, tab, all_x, all_y, out_x, out_y, qx, qy, rx, ry, wx, wy, sem_x, sem_y):
    get_y = fetch(all_y.at[0], wy, sem_y)
    get_x = fetch(all_x.at[0], wx, sem_x)
    get_y.start()
    get_x.start()
    forward_y(field, tab, get_y, wy, out_y, qy, ry)
    forward_x(field, tab, get_x, wx, out_x, qx, rx)


def layer_kernel(layer, last, field, got_x, got_y, tab, up, bias, down, *refs):
    if last:
        result, tmp, lifted = refs
    else:
        all_x, all_y, result, out_x, out_y, tmp, lifted, qx, qy, rx, ry, wx, wy, sem_x, sem_y = refs
        get_y = fetch(all_y.at[layer + 1], wy, sem_y)
        get_x = fetch(all_x.at[layer + 1], wx, sem_x)
        get_y.start()
        get_x.start()
    chans, nx, _ = field.shape
    step = tmp.shape[0] // chans
    add_branches(field, got_x, got_y, tab, tmp)
    feed_forward(layer, up, bias, down, tmp, lifted, nx)
    for c in range(chans):
        result[c] = tmp[c * step : c * step + nx].astype(BF16)
    if not last:
        forward_y(result, tab, get_y, wy, out_y, qy, ry)
        forward_x(result, tab, get_x, wx, out_x, qx, rx)


def call(kernel, outs, scratch, args, flops, far=0):
    vmem = pl.BlockSpec(memory_space=pltpu.VMEM)
    away = pl.BlockSpec(memory_space=pl.ANY)
    return pl.pallas_call(
        kernel,
        out_shape=outs,
        in_specs=[vmem] * (len(args) - far) + [away] * far,
        out_specs=[vmem] * len(outs),
        scratch_shapes=scratch,
        compiler_params=pltpu.CompilerParams(vmem_limit_bytes=24 * 1024 * 1024),
        cost_estimate=pl.CostEstimate(flops=flops, bytes_accessed=4_000_000, transcendentals=0),
    )(*args)


def exchange(cut, axis):
    return lax.all_to_all(cut, axis, split_axis=0, concat_axis=0, tiled=True)


def chunks(parts, axis):
    count = lax.axis_size(axis)
    return parts.reshape(count, parts.shape[0] // count, parts.shape[1])


def total_of(arrived):
    return arrived.astype(F32).sum(axis=0).astype(BF16)


def summed_everywhere(parts_x, parts_y):
    own_y = total_of(exchange(chunks(parts_y, "col"), "col"))
    arrived = exchange(chunks(parts_x, "row"), "row")
    got_y = lax.all_gather(own_y, "col", axis=0, tiled=True)
    copies = jnp.broadcast_to(total_of(arrived), arrived.shape)
    got_x = exchange(copies, "row")
    return got_x.reshape(parts_x.shape), got_y


def on_device(field, x_weight, y_weight, up_weight, up_bias, down_weight):
    _, chans, nx, ny = field.shape
    half = chans // 2
    hid = up_weight.shape[1]
    tab = tables(nx, ny)
    lifts = jnp.swapaxes(up_weight, 1, 2)
    parts = [
        jax.ShapeDtypeStruct((chans * ROWS, ny), BF16),
        jax.ShapeDtypeStruct((half * ROWS, 2 * nx), BF16),
    ]
    whole = jax.ShapeDtypeStruct((chans, nx, ny), BF16)
    work = [
        pltpu.VMEM((ROWS * (chans + PAD), ny), F32),
        pltpu.VMEM((ROWS * (half + PAD), 2 * nx), F32),
        pltpu.VMEM((ROWS * chans, ny), F32),
        pltpu.VMEM((ROWS * half, 2 * nx), F32),
        pltpu.VMEM(x_weight.shape[1:], F32),
        pltpu.VMEM(y_weight.shape[1:], F32),
        pltpu.SemaphoreType.DMA,
        pltpu.SemaphoreType.DMA,
    ]
    space = [pltpu.VMEM((chans * (nx + PAD), ny), F32), pltpu.VMEM((hid, chans + EXTRA), BF16)]
    state = field.reshape(chans, nx, ny)
    first = [state, tab, x_weight, y_weight]
    mx, my = call(first_kernel, parts, work, first, 200_000_000, 2)
    for layer in range(LAYERS):
        last = layer + 1 == LAYERS
        got_x, got_y = summed_everywhere(mx, my)
        got_x = got_x.reshape(chans, ROWS, ny)
        got_y = got_y.reshape(half, ROWS, 2 * nx)
        args = [state, got_x, got_y, tab, lifts, up_bias, down_weight]
        kernel = functools.partial(layer_kernel, layer, last)
        if last:
            (state,) = call(kernel, [whole], space, args, 700_000_000)
        else:
            args += [x_weight, y_weight]
            state, mx, my = call(kernel, [whole, *parts], [*space, *work], args, 900_000_000, 2)
    return state.reshape(field.shape)


def solution(mesh):
    in_specs = (P(None, None, "row", "col"), P(), P(), P(), P(), P())
    out_specs = P(None, None, "row", "col")
    return jax.shard_map(
        on_device, mesh=mesh, in_specs=in_specs, out_specs=out_specs, check_vma=False
    )
```

profile of v0, /device:TPU:1, one launch (start us, length us, event | category | flops | bytes accessed | tf_op | source)
XLA Modules:
  0.0 158.0 jit_solution(13953211875130731820)
XLA Ops:
  0.0 0.1 fusion.16
  0.1 0.1 fusion.14
  0.2 0.1 multiply_convert_fusion
  0.3 0.1 multiply_convert_fusion.1
  0.4 0.1 maximum_maximum_fusion.tab
  0.5 1.4 copy-done
  1.9 1.4 copy-done.2
  3.3 1.2 copy-done.4
  4.5 2.2 %shard_map.64 = (bf16[1536,128]{1,0:T(8,128)(2,1)S(1)}, bf16[768,128]{1,0:T(8,128)(2,1)}) custom-call(bf16[64,64,128]{2,1,0:T(8,128)(2,1)S(1)} %bitcast.11, bf16[72,128]{1,0:T(8,128)(2,1)S(1)} %maximum_maximum_fusion.tab, f32[2,2,12,64,64]{4,3,2,1,0:T(8,128)S(1)} %copy-done, f32[2,2,12,64,64]{4,3,2,1,0:T(8,128)S(1)} %copy-done.2), custom_call_target="tpu_custom_call" | custom-call | flops 200000000 | bytes 4000000 | tf_op jit(solution)/shard_map/pallas_call | solution.py:190
  6.8 27.6 %all_to_all.30 = bf16[32,48,128]{2,1,0:T(8,128)(2,1)S(1)} all-to-all(bf16[32,48,128]{2,1,0:T(8,128)(2,1)S(1)} %bitcast.18), channel_id=1, replica_groups=mesh['row'=32,'col'=16] {'row'}, dimensions={0} | all-to-all | bytes 786432 | tf_op jit(solution)/shard_map/all_to_all | solution.py:202
  34.4 9.5 %all-to-all-start.2 = ((bf16[16,48,128]{2,1,0:T(8,128)(2,1)}), bf16[16,48,128]{2,1,0:T(8,128)(2,1)}, u32[]{:S(2)}, u32[]{:S(2)}) async-start(bf16[16,48,128]{2,1,0:T(8,128)(2,1)} %bitcast.3), calls=%async_computation.2 | async-start | bytes 393216 | tf_op jit(solution)/shard_map/all_to_all | solution.py:202
  43.9 0.1 reduce_sum.48
  44.0 10.2 %all-to-all-done.2 = bf16[16,48,128]{2,1,0:T(8,128)(2,1)} async-done(((bf16[16,48,128]{2,1,0:T(8,128)(2,1)}), bf16[16,48,128]{2,1,0:T(8,128)(2,1)}, u32[]{:S(2)}, u32[]{:S(2)}) %all-to-all-start.2) | async-done | bytes 196640 | tf_op jit(solution)/shard_map/all_to_all | solution.py:202
  54.2 0.8 broadcast_in_dim.24
  55.0 4.0 %all-to-all-start.1 = ((bf16[32,48,128]{2,1,0:T(8,128)(2,1)}), bf16[32,48,128]{2,1,0:T(8,128)(2,1)S(1)}, u32[]{:S(2)}, u32[]{:S(2)}) async-start(bf16[32,48,128]{2,1,0:T(8,128)(2,1)} %broadcast_in_dim.24), calls=%async_computation.1 | async-start | bytes 786432 | tf_op jit(solution)/shard_map/all_to_all | solution.py:202
  59.1 1.0 reduce_sum.49
  60.0 16.5 %all_gather.6 = bf16[768,128]{1,0:T(8,128)(2,1)} all-gather(bf16[48,128]{1,0:T(8,128)(2,1)S(1)} %reduce_sum.49), channel_id=1, replica_groups=mesh['row'=32,'col'=16] {'col'}, dimensions={0}, use_global_device_ids=true | all-gather | bytes 208896 | tf_op jit(solution)/shard_map/all_gather | solution.py:217
  76.6 1.2 copy-done.5
  77.8 0.9 copy-done.8
  78.7 0.7 copy-done.10
  79.5 0.8 copy-done.12
  80.3 0.8 copy-done.14
  81.1 7.9 %shard_map.65 = (bf16[64,64,128]{2,1,0:T(8,128)(2,1)S(1)}, bf16[1536,128]{1,0:T(8,128)(2,1)S(1)}, bf16[768,128]{1,0:T(8,128)(2,1)S(1)}) custom-call(bf16[64,64,128]{2,1,0:T(8,128)(2,1)S(1)} %bitcast.12, bf16[64,24,128]{2,1,0:T(8,128)(2,1)S(1)} %bitcast.13, bf16[32,24,128]{2,1,0:T(8,128)(2,1)S(1)} %bitcast.15, bf16[72,128]{1,0:T(8,128)(2,1)S(1)} %copy-done.10, ...), custom_call_target="tpu_custom_call" | custom-call | flops 900000000 | bytes 4000000 | tf_op jit(solution)/shard_map/pallas_call | solution.py:190
  89.0 1.0 copy-done.6
  90.0 23.8 %all_to_all.31 = bf16[32,48,128]{2,1,0:T(8,128)(2,1)S(1)} all-to-all(bf16[32,48,128]{2,1,0:T(8,128)(2,1)S(1)} %bitcast.17), channel_id=1, replica_groups=mesh['row'=32,'col'=16] {'row'}, dimensions={0} | all-to-all | bytes 786432 | tf_op jit(solution)/shard_map/all_to_all | solution.py:202
  113.8 7.1 %all-to-all-start.5 = ((bf16[16,48,128]{2,1,0:T(8,128)(2,1)}), bf16[16,48,128]{2,1,0:T(8,128)(2,1)S(1)}, u32[]{:S(2)}, u32[]{:S(2)}) async-start(bf16[16,48,128]{2,1,0:T(8,128)(2,1)} %bitcast.21), calls=%async_computation.5 | async-start | bytes 393216 | tf_op jit(solution)/shard_map/all_to_all | solution.py:202
  121.0 0.1 reduce_sum.50
  121.0 10.1 %all-to-all-done.5 = bf16[16,48,128]{2,1,0:T(8,128)(2,1)S(1)} async-done(((bf16[16,48,128]{2,1,0:T(8,128)(2,1)}), bf16[16,48,128]{2,1,0:T(8,128)(2,1)S(1)}, u32[]{:S(2)}, u32[]{:S(2)}) %all-to-all-start.5) | async-done | bytes 196640 | tf_op jit(solution)/shard_map/all_to_all | solution.py:202
  131.2 0.8 broadcast_in_dim.25
  132.0 3.9 %all-to-all-start.4 = ((bf16[32,48,128]{2,1,0:T(8,128)(2,1)}), bf16[32,48,128]{2,1,0:T(8,128)(2,1)S(1)}, u32[]{:S(2)}, u32[]{:S(2)}) async-start(bf16[32,48,128]{2,1,0:T(8,128)(2,1)} %broadcast_in_dim.25), calls=%async_computation.4 | async-start | bytes 786432 | tf_op jit(solution)/shard_map/all_to_all | solution.py:202
  136.0 15.1 %all_gather.7 = bf16[768,128]{1,0:T(8,128)(2,1)S(1)} all-gather(bf16[48,128]{1,0:T(8,128)(2,1)S(1)} %reduce_sum.51), channel_id=1, replica_groups=mesh['row'=32,'col'=16] {'col'}, dimensions={0}, use_global_device_ids=true | all-gather | bytes 208896 | tf_op jit(solution)/shard_map/all_gather | solution.py:217
  151.1 6.9 %shard_map.66 = bf16[64,64,128]{2,1,0:T(8,128)(2,1)} custom-call(bf16[64,64,128]{2,1,0:T(8,128)(2,1)S(1)} %copy-done.7, bf16[64,24,128]{2,1,0:T(8,128)(2,1)S(1)} %bitcast.14, bf16[32,24,128]{2,1,0:T(8,128)(2,1)S(1)} %bitcast.16, bf16[72,128]{1,0:T(8,128)(2,1)S(1)} %copy-done.11, bf16[2,64,256]{2,1,0:T(8,128)(2,1)S(1)} %bitcast.20, f32[2,256]{1,0:T(2,128)S(1)} %copy-done.17, ...), custom_call_target="tpu_custom_call" | custom-call | flops 700000000 | bytes 4000000 | tf_op jit(solution)/shard_map/pallas_call | solution.py:190
  (36 shorter events, 0.2 us)
Async XLA Ops:
  0.5 6.3 %copy-start.9 = (bf16[72,128]{1,0:T(8,128)(2,1)}, bf16[72,128]{1,0:T(8,128)(2,1)S(1)}, u32[]{:S(2)}) copy-start(bf16[72,128]{1,0:T(8,128)(2,1)S(1)} %maximum_maximum_fusion.tab) | copy-start | bytes 55300
  0.5 1.4 copy-start
  1.9 1.4 copy-start.2
  3.3 1.2 copy-start.4
  6.8 69.8 %copy-start.1 = (f32[2,2,12,64,64]{4,3,2,1,0:T(8,128)S(1)}, f32[2,2,12,64,64]{4,3,2,1,0:T(8,128)}, u32[]{:S(2)}) copy-start(f32[2,2,12,64,64]{4,3,2,1,0:T(8,128)} %refs_0_.1) | copy-start | bytes 2359300
  6.8 69.8 %copy-start.3 = (f32[2,2,12,64,64]{4,3,2,1,0:T(8,128)S(1)}, f32[2,2,12,64,64]{4,3,2,1,0:T(8,128)}, u32[]{:S(2)}) copy-start(f32[2,2,12,64,64]{4,3,2,1,0:T(8,128)} %refs_1_.1) | copy-start | bytes 2359300
  6.8 69.8 %copy-start.17 = (f32[2,256]{1,0:T(2,128)S(1)}, f32[2,256]{1,0:T(2,128)}, u32[]{:S(2)}) copy-start(f32[2,256]{1,0:T(2,128)} %bias.3) | copy-start | bytes 6148
  34.4 19.8 %all-to-all-start.2 = ((bf16[16,48,128]{2,1,0:T(8,128)(2,1)}), bf16[16,48,128]{2,1,0:T(8,128)(2,1)}, u32[]{:S(2)}, u32[]{:S(2)}) async-start(bf16[16,48,128]{2,1,0:T(8,128)(2,1)} %bitcast.3), calls=%async_computation.2 | async-start | bytes 393216 | tf_op jit(solution)/shard_map/all_to_all | solution.py:202
  55.0 21.5 %all-to-all-start.1 = ((bf16[32,48,128]{2,1,0:T(8,128)(2,1)}), bf16[32,48,128]{2,1,0:T(8,128)(2,1)S(1)}, u32[]{:S(2)}, u32[]{:S(2)}) async-start(bf16[32,48,128]{2,1,0:T(8,128)(2,1)} %broadcast_in_dim.24), calls=%async_computation.1 | async-start | bytes 786432 | tf_op jit(solution)/shard_map/all_to_all | solution.py:202
  76.6 1.2 copy-start.5
  77.8 0.9 copy-start.8
  78.7 0.7 copy-start.10
  79.5 0.8 copy-start.12
  80.3 0.8 copy-start.14
  89.0 1.0 copy-start.6
  90.0 23.8 %copy-start.16 = (bf16[768,128]{1,0:T(8,128)(2,1)}, bf16[768,128]{1,0:T(8,128)(2,1)S(1)}, u32[]{:S(2)}) copy-start(bf16[768,128]{1,0:T(8,128)(2,1)S(1)} %get-tuple-element.14) | copy-start | bytes 589828
  90.0 61.1 %copy-start.7 = (bf16[64,64,128]{2,1,0:T(8,128)(2,1)S(1)}, bf16[64,64,128]{2,1,0:T(8,128)(2,1)}, u32[]{:S(2)}) copy-start(bf16[64,64,128]{2,1,0:T(8,128)(2,1)} %copy-done.6) | copy-start | bytes 3145732
  90.0 61.1 %copy-start.11 = (bf16[72,128]{1,0:T(8,128)(2,1)S(1)}, bf16[72,128]{1,0:T(8,128)(2,1)}, u32[]{:S(2)}) copy-start(bf16[72,128]{1,0:T(8,128)(2,1)} %copy-done.9) | copy-start | bytes 55300
  90.0 61.1 %copy-start.13 = (bf16[2,256,64]{1,2,0:T(8,128)(2,1)S(1)}, bf16[2,256,64]{1,2,0:T(8,128)(2,1)}, u32[]{:S(2)}) copy-start(bf16[2,256,64]{1,2,0:T(8,128)(2,1)} %param.9) | copy-start | bytes 196612
  90.0 61.1 %copy-start.15 = (bf16[2,64,256]{2,1,0:T(8,128)(2,1)S(1)}, bf16[2,64,256]{2,1,0:T(8,128)(2,1)}, u32[]{:S(2)}) copy-start(bf16[2,64,256]{2,1,0:T(8,128)(2,1)} %down.3) | copy-start | bytes 196612
  113.8 17.3 %all-to-all-start.5 = ((bf16[16,48,128]{2,1,0:T(8,128)(2,1)}), bf16[16,48,128]{2,1,0:T(8,128)(2,1)S(1)}, u32[]{:S(2)}, u32[]{:S(2)}) async-start(bf16[16,48,128]{2,1,0:T(8,128)(2,1)} %bitcast.21), calls=%async_computation.5 | async-start | bytes 393216 | tf_op jit(solution)/shard_map/all_to_all | solution.py:202
  132.0 19.1 %all-to-all-start.4 = ((bf16[32,48,128]{2,1,0:T(8,128)(2,1)}), bf16[32,48,128]{2,1,0:T(8,128)(2,1)S(1)}, u32[]{:S(2)}, u32[]{:S(2)}) async-start(bf16[32,48,128]{2,1,0:T(8,128)(2,1)} %broadcast_in_dim.25), calls=%async_computation.4 | async-start | bytes 786432 | tf_op jit(solution)/shard_map/all_to_all | solution.py:202
where the time goes:
time: 159 us; the launch traced here: 158 us
  blocking collectives  83 us (52%)
  starting transfers between devices  24.6 us (15%)
  waiting for transfers between devices  20.4 us (13%)
  Pallas kernels  17 us (11%)
  local copies, waits for them, and re-layouts  11.2 us (7%)
  other arithmetic  1.6 us (1%)
    all_to_all x2, blocking collectives, exchange(): return lax.all_to_all(cut, axis, split_axis=0, concat_axis=0, tiled=True)  51.4 us
    all_gather x2, blocking collectives, summed_everywhere(): got_y = lax.all_gather(own_y, 'col', axis=0, tiled=True)  31.6 us
    all_to_all x4, starting transfers between devices, exchange(): return lax.all_to_all(cut, axis, split_axis=0, concat_axis=0, tiled=True)  24.6 us
    all_to_all x4, waiting for transfers between devices, exchange(): return lax.all_to_all(cut, axis, split_axis=0, concat_axis=0, tiled=True)  20.4 us
    pallas_call x3, Pallas kernels, call(): pl.pallas_call(kernel, out_shape=outs, in_specs=[vmem] * (len(args) - far...  17 us
    unnamed x36, local copies, waits for them, and re-layouts  9.6 us
  transfers between devices with their start and end apart: 4, of which 2 were waited for; matrix products, arithmetic and copies ran while one was open for 1% of the time, Pallas kernels for 0%

commit v1 on v0

--- a/solution.py
+++ b/solution.py
@@ -18,7 +18,7 @@
 NT = (((1,), (1,)), ((), ()))
 F32, BF16 = jnp.float32, jnp.bfloat16
 BLOCK = 4
-WIDE = 4
+WIDE = 16
 AHEAD = 2
 PAD = 8
 EXTRA = 16
@@ -56,7 +56,7 @@
     return jnp.concatenate([top, bottom], axis=0).astype(BF16)
 
 
-def forward_x(state, tab, got, weight, out, work, laid):
+def forward_x(state, tab, weight, out, work, laid):
     chans, nx, ny = state.shape
     step = work.shape[0] // ROWS
     fwd = tab[2 * ROWS : 3 * ROWS, :nx].astype(F32)
@@ -69,7 +69,6 @@
         part = dot(table, state[c0 : c0 + BLOCK].reshape(BLOCK * nx, ny))
         for i in range(BLOCK):
             put(work, c0 + i, ROWS, step, part[i * ROWS : (i + 1) * ROWS])
-    got.wait()
     for k in range(MODES):
         re = work[k * step : k * step + chans]
         im = work[(MODES + k) * step : (MODES + k) * step + chans]
@@ -79,7 +78,7 @@
     out[...] = laid[...].astype(BF16)
 
 
-def forward_y(state, tab, got, weight, out, work, laid):
+def sums_y(state, tab, work):
     chans, nx, _ = state.shape
     half = chans // 2
     step = work.shape[0] // ROWS
@@ -89,7 +88,12 @@
         part = dot(table, jnp.concatenate(both, axis=0), NT)
         put(work, j, ROWS, step, part[:, : 2 * nx])
         put(work, j + 1, ROWS, step, part[:, 2 * nx :])
-    got.wait()
+
+
+def mix_y(work, weight, out, laid):
+    half, nx = work.shape[0] // ROWS - PAD, work.shape[1] // 2
+    chans = 2 * half
+    step = work.shape[0] // ROWS
     for k in range(MODES):
         re = work[k * step : k * step + half]
         im = work[(MODES + k) * step : (MODES + k) * step + half]
@@ -117,7 +121,7 @@
             tmp[c * step : c * step + nx] = total.astype(F32)
 
 
-def feed_forward(layer, up, bias, down, tmp, lifted, nx):
+def feed_forward(layer, up, bias, down, tmp, lifted, nx, finish):
     _, depth, hid = up.shape
     ny = tmp.shape[1]
     step = tmp.shape[0] // depth
@@ -131,8 +135,7 @@
     lifted[...] = jnp.concatenate(rows, axis=0).T.astype(BF16)
     ones = (lax.broadcasted_iota(jnp.int32, (EXTRA, WIDE * ny), 0) < 3).astype(F32).astype(BF16)
 
-    def feed(i, carry):
-        x0 = i * (WIDE * AHEAD)
+    for x0 in range(0, nx, WIDE * AHEAD):
         wides, news = [], []
         for b in range(AHEAD):
             lines = [tmp[pl.ds(x0 + b * WIDE + a, depth, stride=step), :] for a in range(WIDE)]
@@ -146,52 +149,65 @@
             for a in range(WIDE):
                 line = news[b][:, a * ny : (a + 1) * ny]
                 put(tmp, x0 + b * WIDE + a, depth, step, line)
-        return carry
-
-    lax.fori_loop(0, nx // (WIDE * AHEAD), feed, 0)
+        finish(x0, WIDE * AHEAD)
 
 
 def fetch(source, target, sem):
     return pltpu.make_async_copy(source, target, sem)
 
 
-def first_kernel(field, tab, all_x, all_y, out_x, out_y, qx, qy, rx, ry, wx, wy, sem_x, sem_y):
-    get_y = fetch(all_y.at[0], wy, sem_y)
-    get_x = fetch(all_x.at[0], wx, sem_x)
-    get_y.start()
-    get_x.start()
-    forward_y(field, tab, get_y, wy, out_y, qy, ry)
-    forward_x(field, tab, get_x, wx, out_x, qx, rx)
+def mix_kernel(work, weights, out, laid):
+    mix_y(work, weights.at[0], out, laid)
+
+
+def x_kernel(layer, state, tab, weights, out, work, laid):
+    forward_x(state, tab, weights.at[layer], out, work, laid)
 
 
 def layer_kernel(layer, last, field, got_x, got_y, tab, up, bias, down, *refs):
     if last:
-        result, tmp, lifted = refs
+        result, tmp, lifted, held, sems = refs
     else:
-        all_x, all_y, result, out_x, out_y, tmp, lifted, qx, qy, rx, ry, wx, wy, sem_x, sem_y = refs
-        get_y = fetch(all_y.at[layer + 1], wy, sem_y)
-        get_x = fetch(all_x.at[layer + 1], wx, sem_x)
-        get_y.start()
-        get_x.start()
+        weights, result, out, tmp, lifted, held, sems, work, laid = refs
     chans, nx, _ = field.shape
     step = tmp.shape[0] // chans
     add_branches(field, got_x, got_y, tab, tmp)
-    feed_forward(layer, up, bias, down, tmp, lifted, nx)
-    for c in range(chans):
-        result[c] = tmp[c * step : c * step + nx].astype(BF16)
+    copies = []
+
+    def finish(x0, count):
+        for c in range(chans):
+            row = c * step + x0
+            held[c, x0 : x0 + count, :] = tmp[row : row + count].astype(BF16)
+        lines = pl.ds(x0, count)
+        copy = fetch(held.at[:, lines], result.at[:, lines], sems.at[len(copies)])
+        copy.start()
+        copies.append(copy)
+
+    feed_forward(layer, up, bias, down, tmp, lifted, nx, finish)
     if not last:
-        forward_y(result, tab, get_y, wy, out_y, qy, ry)
-        forward_x(result, tab, get_x, wx, out_x, qx, rx)
-
-
-def call(kernel, outs, scratch, args, flops, far=0):
+        sums_y(held, tab, work)
+        mix_y(work, weights.at[layer + 1], out, laid)
+    for copy in copies:
+        copy.wait()
+
+
+def sum_kernel(arrived, copies):
+    total = arrived[0].astype(F32)
+    for i in range(1, arrived.shape[0]):
+        total = total + arrived[i].astype(F32)
+    total = total.astype(BF16)
+    for i in range(arrived.shape[0]):
+        copies[i] = total
+
+
+def call(kernel, outs, scratch, args, flops, sent=()):
     vmem = pl.BlockSpec(memory_space=pltpu.VMEM)
     away = pl.BlockSpec(memory_space=pl.ANY)
     return pl.pallas_call(
         kernel,
         out_shape=outs,
-        in_specs=[vmem] * (len(args) - far) + [away] * far,
-        out_specs=[vmem] * len(outs),
+        in_specs=[vmem] * len(args),
+        out_specs=[away if i in sent else vmem for i in range(len(outs))],
         scratch_shapes=scratch,
         compiler_params=pltpu.CompilerParams(vmem_limit_bytes=24 * 1024 * 1024),
         cost_estimate=pl.CostEstimate(flops=flops, bytes_accessed=4_000_000, transcendentals=0),
@@ -211,11 +227,13 @@
     return arrived.astype(F32).sum(axis=0).astype(BF16)
 
 
-def summed_everywhere(parts_x, parts_y):
+def summed_everywhere(parts_y, make_x):
     own_y = total_of(exchange(chunks(parts_y, "col"), "col"))
+    parts_x = make_x()
     arrived = exchange(chunks(parts_x, "row"), "row")
     got_y = lax.all_gather(own_y, "col", axis=0, tiled=True)
-    copies = jnp.broadcast_to(total_of(arrived), arrived.shape)
+    shape = jax.ShapeDtypeStruct(arrived.shape, BF16)
+    (copies,) = call(sum_kernel, [shape], [], [arrived], 1_000_000)
     got_x = exchange(copies, "row")
     return got_x.reshape(parts_x.shape), got_y
 
@@ -226,37 +244,43 @@
     hid = up_weight.shape[1]
     tab = tables(nx, ny)
     lifts = jnp.swapaxes(up_weight, 1, 2)
-    parts = [
-        jax.ShapeDtypeStruct((chans * ROWS, ny), BF16),
-        jax.ShapeDtypeStruct((half * ROWS, 2 * nx), BF16),
+    part_x = pltpu.HBM((chans * ROWS, ny), BF16)
+    part_y = pltpu.HBM((half * ROWS, 2 * nx), BF16)
+    whole = pltpu.HBM((chans, nx, ny), BF16)
+    work_x = [
+        pltpu.VMEM((ROWS * (chans + PAD), ny), F32),
+        pltpu.VMEM((ROWS * chans, ny), F32),
     ]
-    whole = jax.ShapeDtypeStruct((chans, nx, ny), BF16)
-    work = [
-        pltpu.VMEM((ROWS * (chans + PAD), ny), F32),
+    work_y = [
         pltpu.VMEM((ROWS * (half + PAD), 2 * nx), F32),
-        pltpu.VMEM((ROWS * chans, ny), F32),
         pltpu.VMEM((ROWS * half, 2 * nx), F32),
-        pltpu.VMEM(x_weight.shape[1:], F32),
-        pltpu.VMEM(y_weight.shape[1:], F32),
-        pltpu.SemaphoreType.DMA,
-        pltpu.SemaphoreType.DMA,
     ]
     space = [pltpu.VMEM((chans * (nx + PAD), ny), F32), pltpu.VMEM((hid, chans + EXTRA), BF16)]
+    one = pltpu.SemaphoreType.DMA
+    space += [pltpu.VMEM((chans, nx, ny), BF16), one((nx // (WIDE * AHEAD),))]
     state = field.reshape(chans, nx, ny)
-    first = [state, tab, x_weight, y_weight]
-    mx, my = call(first_kernel, parts, work, first, 200_000_000, 2)
+    sums = jax.ShapeDtypeStruct(work_y[0].shape, F32)
+    (sums,) = call(sums_y, [sums], [], [state, tab], 60_000_000)
+    (my,) = call(mix_kernel, [part_y], work_y[1:], [sums, y_weight], 40_000_000)
     for layer in range(LAYERS):
         last = layer + 1 == LAYERS
-        got_x, got_y = summed_everywhere(mx, my)
+
+        def make_x(state=state, layer=layer):
+            args = [state, tab, x_weight]
+            kernel = functools.partial(x_kernel, layer)
+            return call(kernel, [part_x], work_x, args, 100_000_000)[0]
+
+        got_x, got_y = summed_everywhere(my, make_x)
         got_x = got_x.reshape(chans, ROWS, ny)
         got_y = got_y.reshape(half, ROWS, 2 * nx)
         args = [state, got_x, got_y, tab, lifts, up_bias, down_weight]
         kernel = functools.partial(layer_kernel, layer, last)
         if last:
-            (state,) = call(kernel, [whole], space, args, 700_000_000)
+            (state,) = call(kernel, [whole], space, args, 700_000_000, sent=(0,))
         else:
-            args += [x_weight, y_weight]
-            state, mx, my = call(kernel, [whole, *parts], [*space, *work], args, 900_000_000, 2)
+            args.append(y_weight)
+            scratch = [*space, *work_y]
+            state, my = call(kernel, [whole, part_y], scratch, args, 900_000_000, sent=(0,))
     return state.reshape(field.shape)
 
 

time: 159 us -> 145 us (0.912)
  blocking collectives: 83 us -> 54.4 us
  starting transfers between devices: 24.6 us -> 38.5 us
  waiting for transfers between devices: 20.4 us -> 30.6 us
  local copies, waits for them, and re-layouts: 11.2 us -> 3.88 us
    all_to_all x2 -> x1, blocking collectives: 51.4 us -> 24 us  [exchange(): return lax.all_to_all(cut, axis, split_axis=0, concat_axis=0, tiled=True)]
    all_to_all x4 -> x5, starting transfers between devices: 24.6 us -> 38.5 us  [exchange(): return lax.all_to_all(cut, axis, split_axis=0, concat_axis=0, tiled=True)]
    all_to_all x4 -> x5, waiting for transfers between devices: 20.4 us -> 30.6 us  [exchange(): return lax.all_to_all(cut, axis, split_axis=0, concat_axis=0, tiled=True)]
    unnamed x36 -> x20, local copies, waits for them, and re-layouts: 9.6 us -> 3.88 us
    broadcast_in_dim x2 -> x0, local copies, waits for them, and re-layouts: 1.6 us -> none  [summed_everywhere(): copies = jnp.broadcast_to(total_of(arrived), arrived.shape)]
    pallas_call x3 -> x8, Pallas kernels: 17 us -> 16 us  [call(): pl.pallas_call(kernel, out_shape=outs, in_specs=[vmem] * len(args), out_s...]
  transfers between devices with their start and end apart: 4 -> 5, of which waited for: 2 -> 3; matrix products, arithmetic and copies ran while one was open for 1% -> 0% of each run, Pallas kernels for 0% -> 3%
where the time goes in v1:
time: 145 us; the launch traced here: 144 us
  blocking collectives  54.4 us (38%)
  starting transfers between devices  38.5 us (27%)
  waiting for transfers between devices  30.6 us (21%)
  Pallas kernels  16 us (11%)
  local copies, waits for them, and re-layouts  3.88 us (3%)
    all_to_all x5, starting transfers between devices, exchange(): return lax.all_to_all(cut, axis, split_axis=0, concat_axis=0, tiled=True)  38.5 us
    all_to_all x5, waiting for transfers between devices, exchange(): return lax.all_to_all(cut, axis, split_axis=0, concat_axis=0, tiled=True)  30.6 us
    all_gather x2, blocking collectives, summed_everywhere(): got_y = lax.all_gather(own_y, 'col', axis=0, tiled=True)  30.4 us
    all_to_all x1, blocking collectives, exchange(): return lax.all_to_all(cut, axis, split_axis=0, concat_axis=0, tiled=True)  24 us
    pallas_call x8, Pallas kernels, call(): pl.pallas_call(kernel, out_shape=outs, in_specs=[vmem] * len(args), out_s...  16 us
    unnamed x20, local copies, waits for them, and re-layouts  3.88 us
  transfers between devices with their start and end apart: 5, of which 3 were waited for; matrix products, arithmetic and copies ran while one was open for 0% of the time, Pallas kernels for 3%

profile of v1, /device:TPU:1, one launch (start us, length us, event | category | flops | bytes accessed | tf_op | source)
XLA Modules:
  0.0 144.2 jit_solution(4267692865963021470)
XLA Ops:
  0.0 0.1 fusion.16
  0.1 0.1 fusion.14
  0.2 0.1 multiply_convert_fusion
  0.3 0.1 fusion.15
  0.3 0.1 multiply_convert_fusion.1
  0.4 0.1 maximum_maximum_fusion.tab
  0.5 1.2 copy-done
  1.7 1.4 copy-done.3
  3.1 1.5 %shard_map.64 = bf16[1536,128]{1,0:T(8,128)(2,1)} custom-call(bf16[64,64,128]{2,1,0:T(8,128)(2,1)S(1)} %bitcast.11, bf16[72,128]{1,0:T(8,128)(2,1)S(1)} %maximum_maximum_fusion.tab, f32[2,2,12,64,64]{4,3,2,1,0:T(8,128)S(1)} %copy-done.3), custom_call_target="tpu_custom_call" | custom-call | flops 100000000 | bytes 4000000 | tf_op jit(solution)/shard_map/pallas_call | solution.py:206
  4.6 13.8 %all-to-all-start = ((bf16[32,48,128]{2,1,0:T(8,128)(2,1)}), bf16[32,48,128]{2,1,0:T(8,128)(2,1)S(1)}, u32[]{:S(2)}, u32[]{:S(2)}) async-start(bf16[32,48,128]{2,1,0:T(8,128)(2,1)} %bitcast.20), calls=%async_computation | async-start | bytes 786432 | tf_op jit(solution)/shard_map/all_to_all | solution.py:218
  18.4 0.5 shard_map.66.work
  18.9 1.5 %shard_map.67 = bf16[768,128]{1,0:T(8,128)(2,1)} custom-call(f32[960,128]{1,0:T(8,128)S(1)} %shard_map.66.work, f32[2,2,12,64,64]{4,3,2,1,0:T(8,128)S(1)} %copy-done.2), custom_call_target="tpu_custom_call" | custom-call | flops 40000000 | bytes 4000000 | tf_op jit(solution)/shard_map/pallas_call | solution.py:206
  20.5 11.8 %all-to-all-done.arrived = bf16[32,48,128]{2,1,0:T(8,128)(2,1)S(1)} async-done(((bf16[32,48,128]{2,1,0:T(8,128)(2,1)}), bf16[32,48,128]{2,1,0:T(8,128)(2,1)S(1)}, u32[]{:S(2)}, u32[]{:S(2)}) %all-to-all-start) | async-done | bytes 393248 | tf_op jit(solution)/shard_map/all_to_all | solution.py:218
  32.3 9.5 %all-to-all-start.2 = ((bf16[16,48,128]{2,1,0:T(8,128)(2,1)}), bf16[16,48,128]{2,1,0:T(8,128)(2,1)S(1)}, u32[]{:S(2)}, u32[]{:S(2)}) async-start(bf16[16,48,128]{2,1,0:T(8,128)(2,1)} %bitcast.22), calls=%async_computation.2 | async-start | bytes 393216 | tf_op jit(solution)/shard_map/all_to_all | solution.py:218
  41.8 0.8 shard_map.65
  42.6 9.4 %all-to-all-done.2 = bf16[16,48,128]{2,1,0:T(8,128)(2,1)S(1)} async-done(((bf16[16,48,128]{2,1,0:T(8,128)(2,1)}), bf16[16,48,128]{2,1,0:T(8,128)(2,1)S(1)}, u32[]{:S(2)}, u32[]{:S(2)}) %all-to-all-start.2) | async-done | bytes 196640 | tf_op jit(solution)/shard_map/all_to_all | solution.py:218
  52.0 4.0 %all-to-all-start.1 = ((bf16[32,48,128]{2,1,0:T(8,128)(2,1)}), bf16[32,48,128]{2,1,0:T(8,128)(2,1)S(1)}, u32[]{:S(2)}, u32[]{:S(2)}) async-start(bf16[32,48,128]{2,1,0:T(8,128)(2,1)} %shard_map.65), calls=%async_computation.1 | async-start | bytes 786432 | tf_op jit(solution)/shard_map/all_to_all | solution.py:218
  56.1 15.1 %all_gather.6 = bf16[768,128]{1,0:T(8,128)(2,1)S(1)} all-gather(bf16[48,128]{1,0:T(8,128)(2,1)S(1)} %reduce_sum.24), channel_id=1, replica_groups=mesh['row'=32,'col'=16] {'col'}, dimensions={0}, use_global_device_ids=true | all-gather | bytes 208896 | tf_op jit(solution)/shard_map/all_gather | solution.py:234
  71.2 0.0 all-to-all-done.1
  71.2 0.0 copy-start.4
  71.2 5.2 %shard_map.68 = (bf16[64,64,128]{2,1,0:T(8,128)(2,1)}, bf16[768,128]{1,0:T(8,128)(2,1)}) custom-call(bf16[64,64,128]{2,1,0:T(8,128)(2,1)S(1)} %bitcast.13, bf16[64,24,128]{2,1,0:T(8,128)(2,1)S(1)} %bitcast.14, bf16[32,24,128]{2,1,0:T(8,128)(2,1)S(1)} %bitcast.16, bf16[72,128]{1,0:T(8,128)(2,1)S(1)} %maximum_maximum_fusion.tab, ...), custom_call_target="tpu_custom_call" | custom-call | flops 900000000 | bytes 4000000 | tf_op jit(solution)/shard_map/pallas_call | solution.py:206
  76.4 0.0 copy-start.5
  76.4 1.2 copy-done.5
  77.6 1.5 %shard_map.69 = bf16[1536,128]{1,0:T(8,128)(2,1)} custom-call(bf16[64,64,128]{2,1,0:T(8,128)(2,1)S(1)} %copy-done.5, bf16[72,128]{1,0:T(8,128)(2,1)S(1)} %maximum_maximum_fusion.tab, f32[2,2,12,64,64]{4,3,2,1,0:T(8,128)S(1)} %copy-done.4), custom_call_target="tpu_custom_call" | custom-call | flops 100000000 | bytes 4000000 | tf_op jit(solution)/shard_map/pallas_call | solution.py:206
  79.1 24.0 %all_to_all.30.arrived = bf16[32,48,128]{2,1,0:T(8,128)(2,1)S(1)} all-to-all(bf16[32,48,128]{2,1,0:T(8,128)(2,1)} %bitcast.21), channel_id=1, replica_groups=mesh['row'=32,'col'=16] {'row'}, dimensions={0} | all-to-all | bytes 786432 | tf_op jit(solution)/shard_map/all_to_all | solution.py:218
  103.1 7.1 %all-to-all-start.5 = ((bf16[16,48,128]{2,1,0:T(8,128)(2,1)}), bf16[16,48,128]{2,1,0:T(8,128)(2,1)S(1)}, u32[]{:S(2)}, u32[]{:S(2)}) async-start(bf16[16,48,128]{2,1,0:T(8,128)(2,1)} %bitcast.8), calls=%async_computation.5 | async-start | bytes 393216 | tf_op jit(solution)/shard_map/all_to_all | solution.py:218
  110.2 0.8 shard_map.70
  111.1 9.4 %all-to-all-done.5 = bf16[16,48,128]{2,1,0:T(8,128)(2,1)S(1)} async-done(((bf16[16,48,128]{2,1,0:T(8,128)(2,1)}), bf16[16,48,128]{2,1,0:T(8,128)(2,1)S(1)}, u32[]{:S(2)}, u32[]{:S(2)}) %all-to-all-start.5) | async-done | bytes 196640 | tf_op jit(solution)/shard_map/all_to_all | solution.py:218
  120.4 3.9 %all-to-all-start.4 = ((bf16[32,48,128]{2,1,0:T(8,128)(2,1)}), bf16[32,48,128]{2,1,0:T(8,128)(2,1)S(1)}, u32[]{:S(2)}, u32[]{:S(2)}) async-start(bf16[32,48,128]{2,1,0:T(8,128)(2,1)} %shard_map.70), calls=%async_computation.4 | async-start | bytes 786432 | tf_op jit(solution)/shard_map/all_to_all | solution.py:218
  124.4 15.3 %all_gather.7 = bf16[768,128]{1,0:T(8,128)(2,1)S(1)} all-gather(bf16[48,128]{1,0:T(8,128)(2,1)S(1)} %reduce_sum.25), channel_id=1, replica_groups=mesh['row'=32,'col'=16] {'col'}, dimensions={0}, use_global_device_ids=true | all-gather | bytes 208896 | tf_op jit(solution)/shard_map/all_gather | solution.py:234
  139.7 0.0 all-to-all-done.4
  139.7 4.3 %shard_map.71 = bf16[64,64,128]{2,1,0:T(8,128)(2,1)} custom-call(bf16[64,64,128]{2,1,0:T(8,128)(2,1)S(1)} %copy-done.6, bf16[64,24,128]{2,1,0:T(8,128)(2,1)S(1)} %bitcast.15, bf16[32,24,128]{2,1,0:T(8,128)(2,1)S(1)} %bitcast.17, bf16[72,128]{1,0:T(8,128)(2,1)S(1)} %maximum_maximum_fusion.tab, bf16[2,64,256]{2,1,0:T(8,128)(2,1)S(1)} %bitcast.19, ...), custom_call_target="tpu_custom_call" | custom-call | flops 700000000 | bytes 4000000 | tf_op jit(solution)/shard_map/pallas_call | solution.py:206
  (22 shorter events, 0.1 us)
Async XLA Ops:
  0.5 1.2 copy-start
  1.7 1.4 copy-start.3
  3.1 15.3 %copy-start.1 = (bf16[1,64,64,128]{3,2,1,0:T(8,128)(2,1)S(1)}, bf16[1,64,64,128]{3,2,1,0:T(8,128)(2,1)}, u32[]{:S(2)}) copy-start(bf16[1,64,64,128]{3,2,1,0:T(8,128)(2,1)} %param.6) | copy-start | bytes 3145732
  4.6 14.3 %copy-start.2 = (f32[2,2,12,64,64]{4,3,2,1,0:T(8,128)S(1)}, f32[2,2,12,64,64]{4,3,2,1,0:T(8,128)}, u32[]{:S(2)}) copy-start(f32[2,2,12,64,64]{4,3,2,1,0:T(8,128)} %refs_0_.1) | copy-start | bytes 2359300
  4.6 27.7 %all-to-all-start = ((bf16[32,48,128]{2,1,0:T(8,128)(2,1)}), bf16[32,48,128]{2,1,0:T(8,128)(2,1)S(1)}, u32[]{:S(2)}, u32[]{:S(2)}) async-start(bf16[32,48,128]{2,1,0:T(8,128)(2,1)} %bitcast.20), calls=%async_computation | async-start | bytes 786432 | tf_op jit(solution)/shard_map/all_to_all | solution.py:218
  20.4 50.8 %copy-start.7 = (bf16[2,256,64]{1,2,0:T(8,128)(2,1)S(1)}, bf16[2,256,64]{1,2,0:T(8,128)(2,1)}, u32[]{:S(2)}) copy-start(bf16[2,256,64]{1,2,0:T(8,128)(2,1)} %param.9) | copy-start | bytes 196612
  20.4 50.8 %copy-start.8 = (bf16[2,64,256]{2,1,0:T(8,128)(2,1)S(1)}, bf16[2,64,256]{2,1,0:T(8,128)(2,1)}, u32[]{:S(2)}) copy-start(bf16[2,64,256]{2,1,0:T(8,128)(2,1)} %down.3) | copy-start | bytes 196612
  20.4 50.8 %copy-start.9 = (f32[2,256]{1,0:T(2,128)S(1)}, f32[2,256]{1,0:T(2,128)}, u32[]{:S(2)}) copy-start(f32[2,256]{1,0:T(2,128)} %bias.3) | copy-start | bytes 6148
  32.3 19.7 %all-to-all-start.2 = ((bf16[16,48,128]{2,1,0:T(8,128)(2,1)}), bf16[16,48,128]{2,1,0:T(8,128)(2,1)S(1)}, u32[]{:S(2)}, u32[]{:S(2)}) async-start(bf16[16,48,128]{2,1,0:T(8,128)(2,1)} %bitcast.22), calls=%async_computation.2 | async-start | bytes 393216 | tf_op jit(solution)/shard_map/all_to_all | solution.py:218
  52.0 19.2 %all-to-all-start.1 = ((bf16[32,48,128]{2,1,0:T(8,128)(2,1)}), bf16[32,48,128]{2,1,0:T(8,128)(2,1)S(1)}, u32[]{:S(2)}, u32[]{:S(2)}) async-start(bf16[32,48,128]{2,1,0:T(8,128)(2,1)} %shard_map.65), calls=%async_computation.1 | async-start | bytes 786432 | tf_op jit(solution)/shard_map/all_to_all | solution.py:218
  71.2 5.2 %copy-start.4 = (f32[2,2,12,64,64]{4,3,2,1,0:T(8,128)S(1)}, f32[2,2,12,64,64]{4,3,2,1,0:T(8,128)}, u32[]{:S(2)}) copy-start(f32[2,2,12,64,64]{4,3,2,1,0:T(8,128)} %weights.5) | copy-start | bytes 2359300
  76.4 1.2 copy-start.5
  79.1 60.6 %copy-start.6 = (bf16[64,64,128]{2,1,0:T(8,128)(2,1)S(1)}, bf16[64,64,128]{2,1,0:T(8,128)(2,1)}, u32[]{:S(2)}) copy-start(bf16[64,64,128]{2,1,0:T(8,128)(2,1)} %get-tuple-element.7.state.field) | copy-start | bytes 3145732
  103.1 17.4 %all-to-all-start.5 = ((bf16[16,48,128]{2,1,0:T(8,128)(2,1)}), bf16[16,48,128]{2,1,0:T(8,128)(2,1)S(1)}, u32[]{:S(2)}, u32[]{:S(2)}) async-start(bf16[16,48,128]{2,1,0:T(8,128)(2,1)} %bitcast.8), calls=%async_computation.5 | async-start | bytes 393216 | tf_op jit(solution)/shard_map/all_to_all | solution.py:218
  120.4 19.3 %all-to-all-start.4 = ((bf16[32,48,128]{2,1,0:T(8,128)(2,1)}), bf16[32,48,128]{2,1,0:T(8,128)(2,1)S(1)}, u32[]{:S(2)}, u32[]{:S(2)}) async-start(bf16[32,48,128]{2,1,0:T(8,128)(2,1)} %shard_map.70), calls=%async_computation.4 | async-start | bytes 786432 | tf_op jit(solution)/shard_map/all_to_all | solution.py:218

commit v2 on v1

--- a/solution.py
+++ b/solution.py
@@ -56,7 +56,7 @@
     return jnp.concatenate([top, bottom], axis=0).astype(BF16)
 
 
-def forward_x(state, tab, weight, out, work, laid):
+def forward_x(state, tab, mixing, weight, out, work, laid):
     chans, nx, ny = state.shape
     step = work.shape[0] // ROWS
     fwd = tab[2 * ROWS : 3 * ROWS, :nx].astype(F32)
@@ -69,6 +69,7 @@
         part = dot(table, state[c0 : c0 + BLOCK].reshape(BLOCK * nx, ny))
         for i in range(BLOCK):
             put(work, c0 + i, ROWS, step, part[i * ROWS : (i + 1) * ROWS])
+    mixing.wait()
     for k in range(MODES):
         re = work[k * step : k * step + chans]
         im = work[(MODES + k) * step : (MODES + k) * step + chans]
@@ -78,7 +79,7 @@
     out[...] = laid[...].astype(BF16)
 
 
-def sums_y(state, tab, work):
+def sums_y(state, tab, out, work):
     chans, nx, _ = state.shape
     half = chans // 2
     step = work.shape[0] // ROWS
@@ -88,17 +89,21 @@
         part = dot(table, jnp.concatenate(both, axis=0), NT)
         put(work, j, ROWS, step, part[:, : 2 * nx])
         put(work, j + 1, ROWS, step, part[:, 2 * nx :])
-
-
-def mix_y(work, weight, out, laid):
-    half, nx = work.shape[0] // ROWS - PAD, work.shape[1] // 2
+    for m in range(ROWS):
+        out[m * half : (m + 1) * half] = work[m * step : m * step + half].astype(BF16)
+
+
+def y_kernel(layer, got, weights, out, laid, weight, sem):
+    mixing = fetch(weights.at[layer], weight, sem)
+    mixing.start()
+    half, nx = got.shape[0] // ROWS, got.shape[1] // 2
     chans = 2 * half
-    step = work.shape[0] // ROWS
+    mixing.wait()
     for k in range(MODES):
-        re = work[k * step : k * step + half]
-        im = work[(MODES + k) * step : (MODES + k) * step + half]
+        re = got[k * half : (k + 1) * half]
+        im = got[(MODES + k) * half : (MODES + k + 1) * half]
         stack = jnp.concatenate([re[:, :nx], re[:, nx:], im[:, :nx], im[:, nx:]], axis=0)
-        mixed = dot(mixer(weight, k), stack.astype(BF16), TN)
+        mixed = dot(mixer(weight, k), stack, TN)
         re = jnp.concatenate([mixed[:half], mixed[half:chans]], axis=1)
         im = jnp.concatenate([mixed[chans : chans + half], mixed[chans + half :]], axis=1)
         put(laid, k, half, ROWS, re)
@@ -156,19 +161,17 @@
     return pltpu.make_async_copy(source, target, sem)
 
 
-def mix_kernel(work, weights, out, laid):
-    mix_y(work, weights.at[0], out, laid)
-
-
-def x_kernel(layer, state, tab, weights, out, work, laid):
-    forward_x(state, tab, weights.at[layer], out, work, laid)
+def x_kernel(layer, state, tab, weights, out, work, laid, weight, sem):
+    mixing = fetch(weights.at[layer], weight, sem)
+    mixing.start()
+    forward_x(state, tab, mixing, weight, out, work, laid)
 
 
 def layer_kernel(layer, last, field, got_x, got_y, tab, up, bias, down, *refs):
     if last:
         result, tmp, lifted, held, sems = refs
     else:
-        weights, result, out, tmp, lifted, held, sems, work, laid = refs
+        result, out, tmp, lifted, held, sems, work = refs
     chans, nx, _ = field.shape
     step = tmp.shape[0] // chans
     add_branches(field, got_x, got_y, tab, tmp)
@@ -185,28 +188,35 @@
 
     feed_forward(layer, up, bias, down, tmp, lifted, nx, finish)
     if not last:
-        sums_y(held, tab, work)
-        mix_y(work, weights.at[layer + 1], out, laid)
+        sums_y(held, tab, out, work)
     for copy in copies:
         copy.wait()
 
 
-def sum_kernel(arrived, copies):
+def summed(arrived):
     total = arrived[0].astype(F32)
     for i in range(1, arrived.shape[0]):
         total = total + arrived[i].astype(F32)
-    total = total.astype(BF16)
+    return total.astype(BF16)
+
+
+def sum_kernel(arrived, out):
+    out[...] = summed(arrived)
+
+
+def copies_kernel(arrived, copies):
+    total = summed(arrived)
     for i in range(arrived.shape[0]):
         copies[i] = total
 
 
-def call(kernel, outs, scratch, args, flops, sent=()):
+def call(kernel, outs, scratch, args, flops, sent=(), far=0):
     vmem = pl.BlockSpec(memory_space=pltpu.VMEM)
     away = pl.BlockSpec(memory_space=pl.ANY)
     return pl.pallas_call(
         kernel,
         out_shape=outs,
-        in_specs=[vmem] * len(args),
+        in_specs=[vmem] * (len(args) - far) + [away] * far,
         out_specs=[away if i in sent else vmem for i in range(len(outs))],
         scratch_shapes=scratch,
         compiler_params=pltpu.CompilerParams(vmem_limit_bytes=24 * 1024 * 1024),
@@ -221,21 +231,6 @@
 def chunks(parts, axis):
     count = lax.axis_size(axis)
     return parts.reshape(count, parts.shape[0] // count, parts.shape[1])
-
-
-def total_of(arrived):
-    return arrived.astype(F32).sum(axis=0).astype(BF16)
-
-
-def summed_everywhere(parts_y, make_x):
-    own_y = total_of(exchange(chunks(parts_y, "col"), "col"))
-    parts_x = make_x()
-    arrived = exchange(chunks(parts_x, "row"), "row")
-    got_y = lax.all_gather(own_y, "col", axis=0, tiled=True)
-    shape = jax.ShapeDtypeStruct(arrived.shape, BF16)
-    (copies,) = call(sum_kernel, [shape], [], [arrived], 1_000_000)
-    got_x = exchange(copies, "row")
-    return got_x.reshape(parts_x.shape), got_y
 
 
 def on_device(field, x_weight, y_weight, up_weight, up_bias, down_weight):
@@ -247,40 +242,44 @@
     part_x = pltpu.HBM((chans * ROWS, ny), BF16)
     part_y = pltpu.HBM((half * ROWS, 2 * nx), BF16)
     whole = pltpu.HBM((chans, nx, ny), BF16)
-    work_x = [
-        pltpu.VMEM((ROWS * (chans + PAD), ny), F32),
-        pltpu.VMEM((ROWS * chans, ny), F32),
+    wide = jax.ShapeDtypeStruct((half * ROWS, 2 * nx), BF16)
+    weight = [pltpu.VMEM(x_weight.shape[1:], F32), pltpu.SemaphoreType.DMA]
+    x_far = pltpu.with_memory_space_constraint(x_weight, pltpu.HBM)
+    y_far = pltpu.with_memory_space_constraint(y_weight, pltpu.HBM)
+    work_x = [pltpu.VMEM((ROWS * (chans + PAD), ny), F32), pltpu.VMEM((ROWS * chans, ny), F32)]
+    work_x += weight
+    work_y = [pltpu.VMEM((ROWS * (half + PAD), 2 * nx), F32)]
+    laid_y = [pltpu.VMEM((ROWS * half, 2 * nx), F32), *weight]
+    space = [
+        pltpu.VMEM((chans * (nx + PAD), ny), F32),
+        pltpu.VMEM((hid, chans + EXTRA), BF16),
+        pltpu.VMEM((chans, nx, ny), BF16),
+        pltpu.SemaphoreType.DMA((nx // (WIDE * AHEAD),)),
     ]
-    work_y = [
-        pltpu.VMEM((ROWS * (half + PAD), 2 * nx), F32),
-        pltpu.VMEM((ROWS * half, 2 * nx), F32),
-    ]
-    space = [pltpu.VMEM((chans * (nx + PAD), ny), F32), pltpu.VMEM((hid, chans + EXTRA), BF16)]
-    one = pltpu.SemaphoreType.DMA
-    space += [pltpu.VMEM((chans, nx, ny), BF16), one((nx // (WIDE * AHEAD),))]
     state = field.reshape(chans, nx, ny)
-    sums = jax.ShapeDtypeStruct(work_y[0].shape, F32)
-    (sums,) = call(sums_y, [sums], [], [state, tab], 60_000_000)
-    (my,) = call(mix_kernel, [part_y], work_y[1:], [sums, y_weight], 40_000_000)
+    (parts_y,) = call(sums_y, [part_y], work_y, [state, tab], 60_000_000)
     for layer in range(LAYERS):
         last = layer + 1 == LAYERS
-
-        def make_x(state=state, layer=layer):
-            args = [state, tab, x_weight]
-            kernel = functools.partial(x_kernel, layer)
-            return call(kernel, [part_x], work_x, args, 100_000_000)[0]
-
-        got_x, got_y = summed_everywhere(my, make_x)
-        got_x = got_x.reshape(chans, ROWS, ny)
-        got_y = got_y.reshape(half, ROWS, 2 * nx)
-        args = [state, got_x, got_y, tab, lifts, up_bias, down_weight]
+        arrived = exchange(chunks(parts_y, "col"), "col")
+        shape = jax.ShapeDtypeStruct(arrived.shape[1:], BF16)
+        (own_y,) = call(sum_kernel, [shape], [], [arrived], 1_000_000)
+        kernel = functools.partial(x_kernel, layer)
+        (parts_x,) = call(kernel, [part_x], work_x, [state, tab, x_far], 100_000_000, far=1)
+        arrived = exchange(chunks(parts_x, "row"), "row")
+        shape = pltpu.HBM(arrived.shape, BF16)
+        (copies,) = call(copies_kernel, [shape], [], [arrived], 1_000_000)
+        got_x = exchange(copies, "row").reshape(chans, ROWS, ny)
+        got_y = lax.all_gather(own_y, "col", axis=0, tiled=True)
+        kernel = functools.partial(y_kernel, layer)
+        (mixed_y,) = call(kernel, [wide], laid_y, [got_y, y_far], 40_000_000, far=1)
+        mixed_y = mixed_y.reshape(half, ROWS, 2 * nx)
+        args = [state, got_x, mixed_y, tab, lifts, up_bias, down_weight]
         kernel = functools.partial(layer_kernel, layer, last)
         if last:
             (state,) = call(kernel, [whole], space, args, 700_000_000, sent=(0,))
         else:
-            args.append(y_weight)
             scratch = [*space, *work_y]
-            state, my = call(kernel, [whole, part_y], scratch, args, 900_000_000, sent=(0,))
+            state, parts_y = call(kernel, [whole, part_y], scratch, args, 900_000_000, sent=(0,))
     return state.reshape(field.shape)
 
 

time: 145 us -> 150 us (1.034)
  Pallas kernels: 16 us -> 21.6 us
    pallas_call x8 -> x11, Pallas kernels: 16 us -> 21.6 us  [call(): pl.pallas_call(kernel, out_shape=outs, in_specs=[vmem] * (len(args) - far...]
    unnamed x20 -> x14, local copies, waits for them, and re-layouts: 3.88 us -> 2.46 us
  transfers between devices with their start and end apart: 5 -> 5, of which waited for: 3 -> 3; matrix products, arithmetic and copies ran while one was open for 0% -> 0% of each run, Pallas kernels for 3% -> 5%
where the time goes in v2:
time: 150 us; the launch traced here: 149 us
  blocking collectives  54.3 us (36%)
  starting transfers between devices  38.3 us (26%)
  waiting for transfers between devices  31.4 us (21%)
  Pallas kernels  21.6 us (14%)
  local copies, waits for them, and re-layouts  2.47 us (2%)
    all_to_all x5, starting transfers between devices, exchange(): return lax.all_to_all(cut, axis, split_axis=0, concat_axis=0, tiled=True)  38.3 us
    all_to_all x5, waiting for transfers between devices, exchange(): return lax.all_to_all(cut, axis, split_axis=0, concat_axis=0, tiled=True)  31.4 us
    all_gather x2, blocking collectives, on_device(): got_y = lax.all_gather(own_y, 'col', axis=0, tiled=True)  30.4 us
    all_to_all x1, blocking collectives, exchange(): return lax.all_to_all(cut, axis, split_axis=0, concat_axis=0, tiled=True)  23.9 us
    pallas_call x11, Pallas kernels, call(): pl.pallas_call(kernel, out_shape=outs, in_specs=[vmem] * (len(args) - far...  21.6 us
  transfers between devices with their start and end apart: 5, of which 3 were waited for; matrix products, arithmetic and copies ran while one was open for 0% of the time, Pallas kernels for 5%

profile of v2, /device:TPU:1, one launch (start us, length us, event | category | flops | bytes accessed | tf_op | source)
XLA Modules:
  0.0 148.9 jit_solution(1250426395784794260)
XLA Ops:
  0.0 0.1 fusion.16
  0.1 0.1 fusion.14
  0.2 0.1 multiply_convert_fusion
  0.3 0.1 fusion.15
  0.3 0.1 multiply_convert_fusion.1
  0.4 0.1 maximum_maximum_fusion.tab
  0.5 1.2 copy-done
  1.7 2.7 %shard_map.64 = bf16[1536,128]{1,0:T(8,128)(2,1)} custom-call(bf16[64,64,128]{2,1,0:T(8,128)(2,1)S(1)} %bitcast.11, bf16[72,128]{1,0:T(8,128)(2,1)S(1)} %maximum_maximum_fusion.tab, f32[2,2,12,64,64]{4,3,2,1,0:T(8,128)} %weights.6), custom_call_target="tpu_custom_call" | custom-call | flops 100000000 | bytes 4000000 | tf_op jit(solution)/shard_map/pallas_call | solution.py:216
  4.4 13.7 %all-to-all-start = ((bf16[32,48,128]{2,1,0:T(8,128)(2,1)}), bf16[32,48,128]{2,1,0:T(8,128)(2,1)S(1)}, u32[]{:S(2)}, u32[]{:S(2)}) async-start(bf16[32,48,128]{2,1,0:T(8,128)(2,1)} %bitcast.20), calls=%async_computation | async-start | bytes 786432 | tf_op jit(solution)/shard_map/all_to_all | solution.py:228
  18.2 0.0 copy-done.1
  18.2 1.2 shard_map.66
  19.3 12.7 %all-to-all-done.arrived = bf16[32,48,128]{2,1,0:T(8,128)(2,1)S(1)} async-done(((bf16[32,48,128]{2,1,0:T(8,128)(2,1)}), bf16[32,48,128]{2,1,0:T(8,128)(2,1)S(1)}, u32[]{:S(2)}, u32[]{:S(2)}) %all-to-all-start) | async-done | bytes 393248 | tf_op jit(solution)/shard_map/all_to_all | solution.py:228
  32.0 9.5 %all-to-all-start.2 = ((bf16[16,48,128]{2,1,0:T(8,128)(2,1)}), bf16[16,48,128]{2,1,0:T(8,128)(2,1)S(1)}, u32[]{:S(2)}, u32[]{:S(2)}) async-start(bf16[16,48,128]{2,1,0:T(8,128)(2,1)} %bitcast.22), calls=%async_computation.2 | async-start | bytes 393216 | tf_op jit(solution)/shard_map/all_to_all | solution.py:228
  41.5 0.8 shard_map.65
  42.3 9.4 %all-to-all-done.2.arrived = bf16[16,48,128]{2,1,0:T(8,128)(2,1)S(1)} async-done(((bf16[16,48,128]{2,1,0:T(8,128)(2,1)}), bf16[16,48,128]{2,1,0:T(8,128)(2,1)S(1)}, u32[]{:S(2)}, u32[]{:S(2)}) %all-to-all-start.2) | async-done | bytes 196640 | tf_op jit(solution)/shard_map/all_to_all | solution.py:228
  51.7 4.0 %all-to-all-start.1 = ((bf16[32,48,128]{2,1,0:T(8,128)(2,1)}), bf16[32,48,128]{2,1,0:T(8,128)(2,1)S(1)}, u32[]{:S(2)}, u32[]{:S(2)}) async-start(bf16[32,48,128]{2,1,0:T(8,128)(2,1)} %shard_map.65), calls=%async_computation.1 | async-start | bytes 786432 | tf_op jit(solution)/shard_map/all_to_all | solution.py:228
  55.8 15.1 %all_gather.6.got = bf16[768,128]{1,0:T(8,128)(2,1)S(1)} all-gather(bf16[48,128]{1,0:T(8,128)(2,1)S(1)} %shard_map.67), channel_id=1, replica_groups=mesh['row'=32,'col'=16] {'col'}, dimensions={0}, use_global_device_ids=true | all-gather | bytes 208896 | tf_op jit(solution)/shard_map/all_gather | solution.py:272
  70.9 2.0 %shard_map.68 = bf16[768,128]{1,0:T(8,128)(2,1)S(1)} custom-call(bf16[768,128]{1,0:T(8,128)(2,1)S(1)} %all_gather.6.got, f32[2,2,12,64,64]{4,3,2,1,0:T(8,128)} %weights.7), custom_call_target="tpu_custom_call" | custom-call | flops 40000000 | bytes 4000000 | tf_op jit(solution)/shard_map/pallas_call | solution.py:216
  72.9 0.0 all-to-all-done.1
  72.9 5.1 %shard_map.69 = (bf16[64,64,128]{2,1,0:T(8,128)(2,1)}, bf16[768,128]{1,0:T(8,128)(2,1)}) custom-call(bf16[64,64,128]{2,1,0:T(8,128)(2,1)S(1)} %bitcast.13, bf16[64,24,128]{2,1,0:T(8,128)(2,1)S(1)} %bitcast.16, bf16[32,24,128]{2,1,0:T(8,128)(2,1)S(1)} %bitcast.17, bf16[72,128]{1,0:T(8,128)(2,1)S(1)} %maximum_maximum_fusion.tab, ...), custom_call_target="tpu_custom_call" | custom-call | flops 900000000 | bytes 4000000 | tf_op jit(solution)/shard_map/pallas_call | solution.py:216
  78.1 0.0 copy-start.2
  78.1 1.2 copy-done.2
  79.3 2.7 %shard_map.70 = bf16[1536,128]{1,0:T(8,128)(2,1)} custom-call(bf16[64,64,128]{2,1,0:T(8,128)(2,1)S(1)} %copy-done.2, bf16[72,128]{1,0:T(8,128)(2,1)S(1)} %maximum_maximum_fusion.tab, f32[2,2,12,64,64]{4,3,2,1,0:T(8,128)} %weights.6), custom_call_target="tpu_custom_call" | custom-call | flops 100000000 | bytes 4000000 | tf_op jit(solution)/shard_map/pallas_call | solution.py:216
  82.0 23.9 %all_to_all.30.arrived = bf16[32,48,128]{2,1,0:T(8,128)(2,1)S(1)} all-to-all(bf16[32,48,128]{2,1,0:T(8,128)(2,1)} %bitcast.21), channel_id=1, replica_groups=mesh['row'=32,'col'=16] {'row'}, dimensions={0} | all-to-all | bytes 786432 | tf_op jit(solution)/shard_map/all_to_all | solution.py:228
  105.8 7.1 %all-to-all-start.5 = ((bf16[16,48,128]{2,1,0:T(8,128)(2,1)}), bf16[16,48,128]{2,1,0:T(8,128)(2,1)S(1)}, u32[]{:S(2)}, u32[]{:S(2)}) async-start(bf16[16,48,128]{2,1,0:T(8,128)(2,1)} %bitcast.8), calls=%async_computation.5 | async-start | bytes 393216 | tf_op jit(solution)/shard_map/all_to_all | solution.py:228
  113.0 0.8 shard_map.71
  113.8 9.4 %all-to-all-done.5.arrived = bf16[16,48,128]{2,1,0:T(8,128)(2,1)S(1)} async-done(((bf16[16,48,128]{2,1,0:T(8,128)(2,1)}), bf16[16,48,128]{2,1,0:T(8,128)(2,1)S(1)}, u32[]{:S(2)}, u32[]{:S(2)}) %all-to-all-start.5) | async-done | bytes 196640 | tf_op jit(solution)/shard_map/all_to_all | solution.py:228
  123.2 3.9 %all-to-all-start.4 = ((bf16[32,48,128]{2,1,0:T(8,128)(2,1)}), bf16[32,48,128]{2,1,0:T(8,128)(2,1)S(1)}, u32[]{:S(2)}, u32[]{:S(2)}) async-start(bf16[32,48,128]{2,1,0:T(8,128)(2,1)} %shard_map.71), calls=%async_computation.4 | async-start | bytes 786432 | tf_op jit(solution)/shard_map/all_to_all | solution.py:228
  127.2 15.3 %all_gather.7.got = bf16[768,128]{1,0:T(8,128)(2,1)S(1)} all-gather(bf16[48,128]{1,0:T(8,128)(2,1)S(1)} %shard_map.72), channel_id=1, replica_groups=mesh['row'=32,'col'=16] {'col'}, dimensions={0}, use_global_device_ids=true | all-gather | bytes 208896 | tf_op jit(solution)/shard_map/all_gather | solution.py:272
  142.5 2.0 %shard_map.73 = bf16[768,128]{1,0:T(8,128)(2,1)S(1)} custom-call(bf16[768,128]{1,0:T(8,128)(2,1)S(1)} %all_gather.7.got, f32[2,2,12,64,64]{4,3,2,1,0:T(8,128)} %weights.7), custom_call_target="tpu_custom_call" | custom-call | flops 40000000 | bytes 4000000 | tf_op jit(solution)/shard_map/pallas_call | solution.py:216
  144.5 0.0 all-to-all-done.4
  144.5 4.3 %shard_map.74 = bf16[64,64,128]{2,1,0:T(8,128)(2,1)} custom-call(bf16[64,64,128]{2,1,0:T(8,128)(2,1)S(1)} %copy-done.3, bf16[64,24,128]{2,1,0:T(8,128)(2,1)S(1)} %bitcast.14, bf16[32,24,128]{2,1,0:T(8,128)(2,1)S(1)} %bitcast.15, bf16[72,128]{1,0:T(8,128)(2,1)S(1)} %maximum_maximum_fusion.tab, bf16[2,64,256]{2,1,0:T(8,128)(2,1)S(1)} %bitcast.19, ...), custom_call_target="tpu_custom_call" | custom-call | flops 700000000 | bytes 4000000 | tf_op jit(solution)/shard_map/pallas_call | solution.py:216
  (17 shorter events, 0.1 us)
Async XLA Ops:
  0.5 1.2 copy-start
  1.7 16.5 %copy-start.1 = (bf16[1,64,64,128]{3,2,1,0:T(8,128)(2,1)S(1)}, bf16[1,64,64,128]{3,2,1,0:T(8,128)(2,1)}, u32[]{:S(2)}) copy-start(bf16[1,64,64,128]{3,2,1,0:T(8,128)(2,1)} %param.6) | copy-start | bytes 3145732
  4.4 27.5 %all-to-all-start = ((bf16[32,48,128]{2,1,0:T(8,128)(2,1)}), bf16[32,48,128]{2,1,0:T(8,128)(2,1)S(1)}, u32[]{:S(2)}, u32[]{:S(2)}) async-start(bf16[32,48,128]{2,1,0:T(8,128)(2,1)} %bitcast.20), calls=%async_computation | async-start | bytes 786432 | tf_op jit(solution)/shard_map/all_to_all | solution.py:228
  32.0 19.7 %all-to-all-start.2 = ((bf16[16,48,128]{2,1,0:T(8,128)(2,1)}), bf16[16,48,128]{2,1,0:T(8,128)(2,1)S(1)}, u32[]{:S(2)}, u32[]{:S(2)}) async-start(bf16[16,48,128]{2,1,0:T(8,128)(2,1)} %bitcast.22), calls=%async_computation.2 | async-start | bytes 393216 | tf_op jit(solution)/shard_map/all_to_all | solution.py:228
  42.3 30.6 %copy-start.4 = (bf16[2,256,64]{1,2,0:T(8,128)(2,1)S(1)}, bf16[2,256,64]{1,2,0:T(8,128)(2,1)}, u32[]{:S(2)}) copy-start(bf16[2,256,64]{1,2,0:T(8,128)(2,1)} %param.9) | copy-start | bytes 196612
  42.3 30.6 %copy-start.5 = (bf16[2,64,256]{2,1,0:T(8,128)(2,1)S(1)}, bf16[2,64,256]{2,1,0:T(8,128)(2,1)}, u32[]{:S(2)}) copy-start(bf16[2,64,256]{2,1,0:T(8,128)(2,1)} %down.3) | copy-start | bytes 196612
  42.3 30.6 %copy-start.6 = (f32[2,256]{1,0:T(2,128)S(1)}, f32[2,256]{1,0:T(2,128)}, u32[]{:S(2)}) copy-start(f32[2,256]{1,0:T(2,128)} %bias.3) | copy-start | bytes 6148
  51.7 21.2 %all-to-all-start.1 = ((bf16[32,48,128]{2,1,0:T(8,128)(2,1)}), bf16[32,48,128]{2,1,0:T(8,128)(2,1)S(1)}, u32[]{:S(2)}, u32[]{:S(2)}) async-start(bf16[32,48,128]{2,1,0:T(8,128)(2,1)} %shard_map.65), calls=%async_computation.1 | async-start | bytes 786432 | tf_op jit(solution)/shard_map/all_to_all | solution.py:228
  78.1 1.2 copy-start.2
  105.8 17.3 %all-to-all-start.5 = ((bf16[16,48,128]{2,1,0:T(8,128)(2,1)}), bf16[16,48,128]{2,1,0:T(8,128)(2,1)S(1)}, u32[]{:S(2)}, u32[]{:S(2)}) async-start(bf16[16,48,128]{2,1,0:T(8,128)(2,1)} %bitcast.8), calls=%async_computation.5 | async-start | bytes 393216 | tf_op jit(solution)/shard_map/all_to_all | solution.py:228
  113.8 30.7 %copy-start.3 = (bf16[64,64,128]{2,1,0:T(8,128)(2,1)S(1)}, bf16[64,64,128]{2,1,0:T(8,128)(2,1)}, u32[]{:S(2)}) copy-start(bf16[64,64,128]{2,1,0:T(8,128)(2,1)} %get-tuple-element.7.state.field) | copy-start | bytes 3145732
  123.2 21.3 %all-to-all-start.4 = ((bf16[32,48,128]{2,1,0:T(8,128)(2,1)}), bf16[32,48,128]{2,1,0:T(8,128)(2,1)S(1)}, u32[]{:S(2)}, u32[]{:S(2)}) async-start(bf16[32,48,128]{2,1,0:T(8,128)(2,1)} %shard_map.71), calls=%async_computation.4 | async-start | bytes 786432 | tf_op jit(solution)/shard_map/all_to_all | solution.py:228

commit v3 on v2

--- a/solution.py
+++ b/solution.py
@@ -53,7 +53,7 @@
     real, imag = weight[0, k], weight[1, k]
     top = jnp.concatenate([real, imag], axis=1)
     bottom = jnp.concatenate([-imag, real], axis=1)
-    return jnp.concatenate([top, bottom], axis=0).astype(BF16)
+    return jnp.concatenate([top, bottom], axis=0)
 
 
 def forward_x(state, tab, mixing, weight, out, work, laid):
@@ -73,7 +73,7 @@
     for k in range(MODES):
         re = work[k * step : k * step + chans]
         im = work[(MODES + k) * step : (MODES + k) * step + chans]
-        mixed = dot(mixer(weight, k), jnp.concatenate([re, im], axis=0).astype(BF16), TN)
+        mixed = dot(mixer(weight, k).astype(BF16), jnp.concatenate([re, im], axis=0).astype(BF16), TN)
         put(laid, k, chans, ROWS, mixed[:chans])
         put(laid, MODES + k, chans, ROWS, mixed[chans:])
     out[...] = laid[...].astype(BF16)
@@ -93,17 +93,14 @@
         out[m * half : (m + 1) * half] = work[m * step : m * step + half].astype(BF16)
 
 
-def y_kernel(layer, got, weights, out, laid, weight, sem):
-    mixing = fetch(weights.at[layer], weight, sem)
-    mixing.start()
+def y_kernel(got, mixers, out, laid):
     half, nx = got.shape[0] // ROWS, got.shape[1] // 2
     chans = 2 * half
-    mixing.wait()
     for k in range(MODES):
         re = got[k * half : (k + 1) * half]
         im = got[(MODES + k) * half : (MODES + k + 1) * half]
         stack = jnp.concatenate([re[:, :nx], re[:, nx:], im[:, :nx], im[:, nx:]], axis=0)
-        mixed = dot(mixer(weight, k), stack, TN)
+        mixed = dot(mixers[k], stack)
         re = jnp.concatenate([mixed[:half], mixed[half:chans]], axis=1)
         im = jnp.concatenate([mixed[chans : chans + half], mixed[chans + half :]], axis=1)
         put(laid, k, half, ROWS, re)
@@ -161,10 +158,15 @@
     return pltpu.make_async_copy(source, target, sem)
 
 
-def x_kernel(layer, state, tab, weights, out, work, laid, weight, sem):
-    mixing = fetch(weights.at[layer], weight, sem)
+def x_kernel(layer, state, tab, all_x, all_y, out, mixers, work, laid, weight, other, sems):
+    mixing = fetch(all_x.at[layer], weight, sems.at[0])
     mixing.start()
+    later = fetch(all_y.at[layer], other, sems.at[1])
+    later.start()
     forward_x(state, tab, mixing, weight, out, work, laid)
+    later.wait()
+    for k in range(MODES):
+        mixers[k] = mixer(other, k).T.astype(BF16)
 
 
 def layer_kernel(layer, last, field, got_x, got_y, tab, up, bias, down, *refs):
@@ -243,13 +245,14 @@
     part_y = pltpu.HBM((half * ROWS, 2 * nx), BF16)
     whole = pltpu.HBM((chans, nx, ny), BF16)
     wide = jax.ShapeDtypeStruct((half * ROWS, 2 * nx), BF16)
-    weight = [pltpu.VMEM(x_weight.shape[1:], F32), pltpu.SemaphoreType.DMA]
+    mixers = jax.ShapeDtypeStruct((MODES, 2 * chans, 2 * chans), BF16)
     x_far = pltpu.with_memory_space_constraint(x_weight, pltpu.HBM)
     y_far = pltpu.with_memory_space_constraint(y_weight, pltpu.HBM)
     work_x = [pltpu.VMEM((ROWS * (chans + PAD), ny), F32), pltpu.VMEM((ROWS * chans, ny), F32)]
-    work_x += weight
+    work_x += [pltpu.VMEM(x_weight.shape[1:], F32), pltpu.VMEM(y_weight.shape[1:], F32)]
+    work_x.append(pltpu.SemaphoreType.DMA((2,)))
     work_y = [pltpu.VMEM((ROWS * (half + PAD), 2 * nx), F32)]
-    laid_y = [pltpu.VMEM((ROWS * half, 2 * nx), F32), *weight]
+    laid_y = [pltpu.VMEM((ROWS * half, 2 * nx), F32)]
     space = [
         pltpu.VMEM((chans * (nx + PAD), ny), F32),
         pltpu.VMEM((hid, chans + EXTRA), BF16),
@@ -264,14 +267,14 @@
         shape = jax.ShapeDtypeStruct(arrived.shape[1:], BF16)
         (own_y,) = call(sum_kernel, [shape], [], [arrived], 1_000_000)
         kernel = functools.partial(x_kernel, layer)
-        (parts_x,) = call(kernel, [part_x], work_x, [state, tab, x_far], 100_000_000, far=1)
+        args = [state, tab, x_far, y_far]
+        parts_x, mix_y = call(kernel, [part_x, mixers], work_x, args, 100_000_000, far=2)
         arrived = exchange(chunks(parts_x, "row"), "row")
         shape = pltpu.HBM(arrived.shape, BF16)
         (copies,) = call(copies_kernel, [shape], [], [arrived], 1_000_000)
         got_x = exchange(copies, "row").reshape(chans, ROWS, ny)
         got_y = lax.all_gather(own_y, "col", axis=0, tiled=True)
-        kernel = functools.partial(y_kernel, layer)
-        (mixed_y,) = call(kernel, [wide], laid_y, [got_y, y_far], 40_000_000, far=1)
+        (mixed_y,) = call(y_kernel, [wide], laid_y, [got_y, mix_y], 40_000_000)
         mixed_y = mixed_y.reshape(half, ROWS, 2 * nx)
         args = [state, got_x, mixed_y, tab, lifts, up_bias, down_weight]
         kernel = functools.partial(layer_kernel, layer, last)

time: 150 us -> 147 us (0.980)
  Pallas kernels: 21.6 us -> 18.5 us
    pallas_call x11, Pallas kernels: 21.6 us -> 18.5 us  [call(): pl.pallas_call(kernel, out_shape=outs, in_specs=[vmem] * (len(args) - far...]
  transfers between devices with their start and end apart: 5 -> 5, of which waited for: 3 -> 3; matrix products, arithmetic and copies ran while one was open for 0% -> 0% of each run, Pallas kernels for 5% -> 3%
where the time goes in v3:
time: 147 us; the launch traced here: 146 us
  blocking collectives  54.3 us (37%)
  starting transfers between devices  38.6 us (26%)
  waiting for transfers between devices  31.4 us (21%)
  Pallas kernels  18.5 us (13%)
  local copies, waits for them, and re-layouts  2.47 us (2%)
    all_to_all x5, starting transfers between devices, exchange(): return lax.all_to_all(cut, axis, split_axis=0, concat_axis=0, tiled=True)  38.6 us
    all_to_all x5, waiting for transfers between devices, exchange(): return lax.all_to_all(cut, axis, split_axis=0, concat_axis=0, tiled=True)  31.4 us
    all_gather x2, blocking collectives, on_device(): got_y = lax.all_gather(own_y, 'col', axis=0, tiled=True)  30.4 us
    all_to_all x1, blocking collectives, exchange(): return lax.all_to_all(cut, axis, split_axis=0, concat_axis=0, tiled=True)  23.9 us
    pallas_call x11, Pallas kernels, call(): pl.pallas_call(kernel, out_shape=outs, in_specs=[vmem] * (len(args) - far...  18.5 us
  transfers between devices with their start and end apart: 5, of which 3 were waited for; matrix products, arithmetic and copies ran while one was open for 0% of the time, Pallas kernels for 3%

profile of v3, /device:TPU:1, one launch (start us, length us, event | category | flops | bytes accessed | tf_op | source)
XLA Modules:
  0.0 146.1 jit_solution(121547031486339290)
XLA Ops:
  0.0 0.1 fusion.16
  0.1 0.1 fusion.14
  0.2 0.1 multiply_convert_fusion
  0.3 0.1 fusion.15
  0.3 0.1 multiply_convert_fusion.1
  0.4 0.1 maximum_maximum_fusion.tab
  0.5 1.2 copy-done
  1.7 2.7 %shard_map.64 = (bf16[1536,128]{1,0:T(8,128)(2,1)}, bf16[12,128,128]{2,1,0:T(8,128)(2,1)S(1)}) custom-call(bf16[64,64,128]{2,1,0:T(8,128)(2,1)S(1)} %bitcast.11, bf16[72,128]{1,0:T(8,128)(2,1)S(1)} %maximum_maximum_fusion.tab, f32[2,2,12,64,64]{4,3,2,1,0:T(8,128)} %all_x.3, f32[2,2,12,64,64]{4,3,2,1,0:T(8,128)} %all_y.3), custom_call_target="tpu_custom_call" | custom-call | flops 100000000 | bytes 4000000 | tf_op jit(solution)/shard_map/pallas_call | solution.py:218
  4.5 13.7 %all-to-all-start = ((bf16[32,48,128]{2,1,0:T(8,128)(2,1)}), bf16[32,48,128]{2,1,0:T(8,128)(2,1)S(1)}, u32[]{:S(2)}, u32[]{:S(2)}) async-start(bf16[32,48,128]{2,1,0:T(8,128)(2,1)} %bitcast.21), calls=%async_computation | async-start | bytes 786432 | tf_op jit(solution)/shard_map/all_to_all | solution.py:230
  18.2 0.0 copy-done.1
  18.2 1.1 shard_map.66
  19.3 12.7 %all-to-all-done.arrived = bf16[32,48,128]{2,1,0:T(8,128)(2,1)S(1)} async-done(((bf16[32,48,128]{2,1,0:T(8,128)(2,1)}), bf16[32,48,128]{2,1,0:T(8,128)(2,1)S(1)}, u32[]{:S(2)}, u32[]{:S(2)}) %all-to-all-start) | async-done | bytes 393248 | tf_op jit(solution)/shard_map/all_to_all | solution.py:230
  32.0 9.7 %all-to-all-start.2 = ((bf16[16,48,128]{2,1,0:T(8,128)(2,1)}), bf16[16,48,128]{2,1,0:T(8,128)(2,1)S(1)}, u32[]{:S(2)}, u32[]{:S(2)}) async-start(bf16[16,48,128]{2,1,0:T(8,128)(2,1)} %bitcast.20), calls=%async_computation.2 | async-start | bytes 393216 | tf_op jit(solution)/shard_map/all_to_all | solution.py:230
  41.7 0.8 shard_map.65
  42.5 9.4 %all-to-all-done.2.arrived = bf16[16,48,128]{2,1,0:T(8,128)(2,1)S(1)} async-done(((bf16[16,48,128]{2,1,0:T(8,128)(2,1)}), bf16[16,48,128]{2,1,0:T(8,128)(2,1)S(1)}, u32[]{:S(2)}, u32[]{:S(2)}) %all-to-all-start.2) | async-done | bytes 196640 | tf_op jit(solution)/shard_map/all_to_all | solution.py:230
  51.9 4.0 %all-to-all-start.1 = ((bf16[32,48,128]{2,1,0:T(8,128)(2,1)}), bf16[32,48,128]{2,1,0:T(8,128)(2,1)S(1)}, u32[]{:S(2)}, u32[]{:S(2)}) async-start(bf16[32,48,128]{2,1,0:T(8,128)(2,1)} %shard_map.65), calls=%async_computation.1 | async-start | bytes 786432 | tf_op jit(solution)/shard_map/all_to_all | solution.py:230
  55.9 15.1 %all_gather.6.got = bf16[768,128]{1,0:T(8,128)(2,1)S(1)} all-gather(bf16[48,128]{1,0:T(8,128)(2,1)S(1)} %shard_map.67), channel_id=1, replica_groups=mesh['row'=32,'col'=16] {'col'}, dimensions={0}, use_global_device_ids=true | all-gather | bytes 208896 | tf_op jit(solution)/shard_map/all_gather | solution.py:276
  71.1 0.4 shard_map.68
  71.5 0.0 all-to-all-done.1
  71.5 5.1 %shard_map.69 = (bf16[64,64,128]{2,1,0:T(8,128)(2,1)}, bf16[768,128]{1,0:T(8,128)(2,1)}) custom-call(bf16[64,64,128]{2,1,0:T(8,128)(2,1)S(1)} %bitcast.13, bf16[64,24,128]{2,1,0:T(8,128)(2,1)S(1)} %bitcast.16, bf16[32,24,128]{2,1,0:T(8,128)(2,1)S(1)} %bitcast.17, bf16[72,128]{1,0:T(8,128)(2,1)S(1)} %maximum_maximum_fusion.tab, ...), custom_call_target="tpu_custom_call" | custom-call | flops 900000000 | bytes 4000000 | tf_op jit(solution)/shard_map/pallas_call | solution.py:218
  76.6 0.0 copy-start.2
  76.7 1.2 copy-done.2
  77.9 2.7 %shard_map.70 = (bf16[1536,128]{1,0:T(8,128)(2,1)}, bf16[12,128,128]{2,1,0:T(8,128)(2,1)S(1)}) custom-call(bf16[64,64,128]{2,1,0:T(8,128)(2,1)S(1)} %copy-done.2, bf16[72,128]{1,0:T(8,128)(2,1)S(1)} %maximum_maximum_fusion.tab, f32[2,2,12,64,64]{4,3,2,1,0:T(8,128)} %all_x.3, f32[2,2,12,64,64]{4,3,2,1,0:T(8,128)} %all_y.3), custom_call_target="tpu_custom_call" | custom-call | flops 100000000 | bytes 4000000 | tf_op jit(solution)/shard_map/pallas_call | solution.py:218
  80.5 23.9 %all_to_all.30.arrived = bf16[32,48,128]{2,1,0:T(8,128)(2,1)S(1)} all-to-all(bf16[32,48,128]{2,1,0:T(8,128)(2,1)} %bitcast.22), channel_id=1, replica_groups=mesh['row'=32,'col'=16] {'row'}, dimensions={0} | all-to-all | bytes 786432 | tf_op jit(solution)/shard_map/all_to_all | solution.py:230
  104.4 7.2 %all-to-all-start.5 = ((bf16[16,48,128]{2,1,0:T(8,128)(2,1)}), bf16[16,48,128]{2,1,0:T(8,128)(2,1)S(1)}, u32[]{:S(2)}, u32[]{:S(2)}) async-start(bf16[16,48,128]{2,1,0:T(8,128)(2,1)} %bitcast.8), calls=%async_computation.5 | async-start | bytes 393216 | tf_op jit(solution)/shard_map/all_to_all | solution.py:230
  111.7 0.8 shard_map.71
  112.5 9.4 %all-to-all-done.5.arrived = bf16[16,48,128]{2,1,0:T(8,128)(2,1)S(1)} async-done(((bf16[16,48,128]{2,1,0:T(8,128)(2,1)}), bf16[16,48,128]{2,1,0:T(8,128)(2,1)S(1)}, u32[]{:S(2)}, u32[]{:S(2)}) %all-to-all-start.5) | async-done | bytes 196640 | tf_op jit(solution)/shard_map/all_to_all | solution.py:230
  121.9 3.9 %all-to-all-start.4 = ((bf16[32,48,128]{2,1,0:T(8,128)(2,1)}), bf16[32,48,128]{2,1,0:T(8,128)(2,1)S(1)}, u32[]{:S(2)}, u32[]{:S(2)}) async-start(bf16[32,48,128]{2,1,0:T(8,128)(2,1)} %shard_map.71), calls=%async_computation.4 | async-start | bytes 786432 | tf_op jit(solution)/shard_map/all_to_all | solution.py:230
  125.9 15.3 %all_gather.7.got = bf16[768,128]{1,0:T(8,128)(2,1)S(1)} all-gather(bf16[48,128]{1,0:T(8,128)(2,1)S(1)} %shard_map.72), channel_id=1, replica_groups=mesh['row'=32,'col'=16] {'col'}, dimensions={0}, use_global_device_ids=true | all-gather | bytes 208896 | tf_op jit(solution)/shard_map/all_gather | solution.py:276
  141.2 0.4 shard_map.73
  141.6 0.0 all-to-all-done.4
  141.6 4.3 %shard_map.74 = bf16[64,64,128]{2,1,0:T(8,128)(2,1)} custom-call(bf16[64,64,128]{2,1,0:T(8,128)(2,1)S(1)} %copy-done.3, bf16[64,24,128]{2,1,0:T(8,128)(2,1)S(1)} %bitcast.14, bf16[32,24,128]{2,1,0:T(8,128)(2,1)S(1)} %bitcast.15, bf16[72,128]{1,0:T(8,128)(2,1)S(1)} %maximum_maximum_fusion.tab, bf16[2,64,256]{2,1,0:T(8,128)(2,1)S(1)} %bitcast.19, ...), custom_call_target="tpu_custom_call" | custom-call | flops 700000000 | bytes 4000000 | tf_op jit(solution)/shard_map/pallas_call | solution.py:218
  (17 shorter events, 0.1 us)
Async XLA Ops:
  0.5 1.2 copy-start
  1.7 16.5 %copy-start.1 = (bf16[1,64,64,128]{3,2,1,0:T(8,128)(2,1)S(1)}, bf16[1,64,64,128]{3,2,1,0:T(8,128)(2,1)}, u32[]{:S(2)}) copy-start(bf16[1,64,64,128]{3,2,1,0:T(8,128)(2,1)} %param.6) | copy-start | bytes 3145732
  4.5 27.5 %all-to-all-start = ((bf16[32,48,128]{2,1,0:T(8,128)(2,1)}), bf16[32,48,128]{2,1,0:T(8,128)(2,1)S(1)}, u32[]{:S(2)}, u32[]{:S(2)}) async-start(bf16[32,48,128]{2,1,0:T(8,128)(2,1)} %bitcast.21), calls=%async_computation | async-start | bytes 786432 | tf_op jit(solution)/shard_map/all_to_all | solution.py:230
  32.0 39.5 %copy-start.4 = (bf16[2,256,64]{1,2,0:T(8,128)(2,1)S(1)}, bf16[2,256,64]{1,2,0:T(8,128)(2,1)}, u32[]{:S(2)}) copy-start(bf16[2,256,64]{1,2,0:T(8,128)(2,1)} %param.9) | copy-start | bytes 196612
  32.0 39.5 %copy-start.5 = (bf16[2,64,256]{2,1,0:T(8,128)(2,1)S(1)}, bf16[2,64,256]{2,1,0:T(8,128)(2,1)}, u32[]{:S(2)}) copy-start(bf16[2,64,256]{2,1,0:T(8,128)(2,1)} %down.3) | copy-start | bytes 196612
  32.0 39.5 %copy-start.6 = (f32[2,256]{1,0:T(2,128)S(1)}, f32[2,256]{1,0:T(2,128)}, u32[]{:S(2)}) copy-start(f32[2,256]{1,0:T(2,128)} %bias.3) | copy-start | bytes 6148
  32.0 19.9 %all-to-all-start.2 = ((bf16[16,48,128]{2,1,0:T(8,128)(2,1)}), bf16[16,48,128]{2,1,0:T(8,128)(2,1)S(1)}, u32[]{:S(2)}, u32[]{:S(2)}) async-start(bf16[16,48,128]{2,1,0:T(8,128)(2,1)} %bitcast.20), calls=%async_computation.2 | async-start | bytes 393216 | tf_op jit(solution)/shard_map/all_to_all | solution.py:230
  51.9 19.6 %all-to-all-start.1 = ((bf16[32,48,128]{2,1,0:T(8,128)(2,1)}), bf16[32,48,128]{2,1,0:T(8,128)(2,1)S(1)}, u32[]{:S(2)}, u32[]{:S(2)}) async-start(bf16[32,48,128]{2,1,0:T(8,128)(2,1)} %shard_map.65), calls=%async_computation.1 | async-start | bytes 786432 | tf_op jit(solution)/shard_map/all_to_all | solution.py:230
  76.6 1.2 copy-start.2
  104.4 37.2 %copy-start.3 = (bf16[64,64,128]{2,1,0:T(8,128)(2,1)S(1)}, bf16[64,64,128]{2,1,0:T(8,128)(2,1)}, u32[]{:S(2)}) copy-start(bf16[64,64,128]{2,1,0:T(8,128)(2,1)} %get-tuple-element.13.state.field) | copy-start | bytes 3145732
  104.4 17.4 %all-to-all-start.5 = ((bf16[16,48,128]{2,1,0:T(8,128)(2,1)}), bf16[16,48,128]{2,1,0:T(8,128)(2,1)S(1)}, u32[]{:S(2)}, u32[]{:S(2)}) async-start(bf16[16,48,128]{2,1,0:T(8,128)(2,1)} %bitcast.8), calls=%async_computation.5 | async-start | bytes 393216 | tf_op jit(solution)/shard_map/all_to_all | solution.py:230
  121.9 19.7 %all-to-all-start.4 = ((bf16[32,48,128]{2,1,0:T(8,128)(2,1)}), bf16[32,48,128]{2,1,0:T(8,128)(2,1)S(1)}, u32[]{:S(2)}, u32[]{:S(2)}) async-start(bf16[32,48,128]{2,1,0:T(8,128)(2,1)} %shard_map.71), calls=%async_computation.4 | async-start | bytes 786432 | tf_op jit(solution)/shard_map/all_to_all | solution.py:230
